TPU v7x, 768 devices: a whole 4x8x12 slice. The times are simulated.
768 devices in a mesh: gx: 12 (over z), gy: 16 (over y_lo, x, core), gz: 4 (over y_hi).
Axes of the slice: x: 4, y: 8 (y_hi: 4, y_lo: 2; y = y_hi * 2 + y_lo), z: 12, core: 2. Of those that a mesh axis runs over, the one named last changes fastest.
Arguments:
- hidden_in: bfloat16 [24576, 4096], P(('gx', 'gy'), 'gz'), may hold values from -40 to 40
- norm_gain: float32 [4096], P('gz'), may hold values from 0.25 to 1.75
- normed_grad: bfloat16 [24576, 4096], P(('gx', 'gy'), 'gz'), may hold values from -64 to 64
- key_grad: bfloat16 [24576, 512], P(('gx', 'gy')), may hold values from -6 to 6
- weight_blocks: bfloat16 [192, 4, 29, 128], P(('gx', 'gy'), 'gz'), may hold values from -0.09375 to 0.09375
- block_count: int32 [4, 192], P('gz'), may hold values from 1 to 29, as said below
Outputs:
- hidden_grad: bfloat16 [24576, 4096], P(('gx', 'gy'), 'gz')
- weight_grad: float32 [192, 4, 29, 128], P(('gx', 'gy'), 'gz')
Inputs may be any that keep to these rules, and one draw needn't show every extreme that they name: `block_count`: each row sums to 4096; in each row the owners i * 16 to i * 16 + 15 hold together exactly the blocks i * 342 to min((i + 1) * 342, 4096) - 1, and one of them holds exactly 29 blocks.
All inputs are finite; a program needn't handle non-finite values.
Results may differ from a plain program's by a relative error of at most 0.0029.
Values may be sent and summed in bfloat16 or wider, within the bound.
A program may use at most 32 MiB of HBM per device.

v0:
```python
import jax
import jax.numpy as jnp
from jax import lax
from jax.sharding import PartitionSpec as P

EPS = 1e-06


def sent_to_all(shard, axis):
    count = lax.axis_size(axis)
    return lax.all_to_all(
        jnp.broadcast_to(shard[None], (count, *shard.shape)), axis, 0, 0, tiled=True
    )


def of_everyone(shard, axis):
    everything = sent_to_all(shard, axis)
    return jnp.sum(everything, axis=0)


def cut_along(shard, dim, count):
    before, after = (shard.shape[:dim], shard.shape[dim + 1 :])
    return jnp.moveaxis(shard.reshape(*before, count, -1, *after), dim, 0)


def summed_on_arrival(shard, axis, dim):
    blocks = cut_along(shard, dim, lax.axis_size(axis))
    arrived = lax.all_to_all(blocks, axis, split_axis=0, concat_axis=0, tiled=True)
    return arrived.sum(axis=0)


def block_layout(counts, blocks, owners, most):
    ends = jnp.cumsum(counts)
    starts = ends - counts
    block_ids = jnp.arange(blocks, dtype=jnp.int32)
    owner = jnp.searchsorted(ends, block_ids, side="right")
    gather_index = owner * most + block_ids - starts[owner]
    slot_owner = jnp.arange(owners * most, dtype=jnp.int32) // most
    slot_within = jnp.arange(owners * most, dtype=jnp.int32) % most
    valid = slot_within < counts[slot_owner]
    source = jnp.clip(starts[slot_owner] + slot_within, 0, blocks - 1)
    return (gather_index, source, valid)


def select_rows(index, keep, rows):
    columns = jnp.arange(rows.shape[0], dtype=jnp.int32)
    onehot = (index[:, None] == columns[None, :]) & keep[:, None]
    if rows.dtype == jnp.bfloat16:
        picked = jnp.dot(onehot.astype(jnp.bfloat16), rows, preferred_element_type=jnp.float32)
        return picked.astype(jnp.bfloat16)
    return jnp.dot(
        onehot.astype(jnp.float32),
        rows,
        precision=lax.Precision.HIGHEST,
        preferred_element_type=jnp.float32,
    )


def select_groups(index, keep, rows):

    def one_group(items):
        return select_rows(items[0], items[1], items[2])

    return lax.map(one_group, (index, keep, rows))


def shards(hidden_in, norm_gain, normed_grad, key_grad, weight_blocks, block_count):
    outer_size = lax.axis_size("gx")
    inner_size = lax.axis_size("gy")
    owners = outer_size * inner_size
    most = weight_blocks.shape[2]
    group_slots_count = inner_size * most
    group_rows = hidden_in.shape[1]
    width = key_grad.shape[1]
    blocks = group_rows * width // 128
    group_blocks = (blocks + outer_size - 1) // outer_size
    model_width = group_rows * lax.axis_size("gz")
    gather_index, source, valid = block_layout(block_count[0], blocks, owners, most)
    outer_index = lax.axis_index("gx")
    padded_index = jnp.pad(gather_index, (0, outer_size * group_blocks - blocks), mode="edge")
    group_offsets = jnp.arange(outer_size, dtype=jnp.int32)[:, None]
    local_index = jnp.clip(
        padded_index.reshape(outer_size, group_blocks) - group_offsets * group_slots_count,
        0,
        group_slots_count - 1,
    )
    local_source = jnp.clip(
        source.reshape(outer_size, group_slots_count) - group_offsets * group_blocks,
        0,
        group_blocks - 1,
    )
    local_valid = valid.reshape(outer_size, group_slots_count)
    all_rows = jnp.ones((outer_size, group_blocks), dtype=bool)
    local_blocks = weight_blocks.reshape(most, 128)
    gathered = lax.all_gather(local_blocks, ("gx", "gy"), axis=0, tiled=True)
    dense = select_groups(
        local_index, all_rows, gathered.reshape(outer_size, group_slots_count, 128)
    )
    weight = dense.reshape(outer_size * group_blocks, 128)[:blocks].reshape(group_rows, width)
    hfloat = hidden_in.astype(jnp.float32)
    squares = of_everyone(jnp.sum(hfloat * hfloat, axis=1), "gz")
    rstd = lax.rsqrt(squares / model_width + EPS)
    normed = (hfloat * rstd[:, None] * norm_gain).astype(jnp.bfloat16)
    dnorm = normed_grad.astype(jnp.float32) + lax.dot_general(
        key_grad, weight, (((1,), (1,)), ((), ())), preferred_element_type=jnp.float32
    )
    proj = of_everyone(jnp.sum(norm_gain * dnorm * hfloat, axis=1), "gz")
    grad = norm_gain * dnorm * rstd[:, None] - hfloat * (rstd**3 * proj / model_width)[:, None]
    hidden_grad = grad.astype(jnp.bfloat16)
    dweight = lax.dot_general(
        normed, key_grad, (((0,), (0,)), ((), ())), preferred_element_type=jnp.float32
    )
    flat = dweight.reshape(blocks, 128)
    flat_padded = jnp.pad(flat, ((0, outer_size * group_blocks - blocks), (0, 0)))
    group_sum = summed_on_arrival(flat_padded, "gx", 0)
    slot_source = lax.dynamic_index_in_dim(local_source, outer_index, 0, keepdims=False)
    slot_valid = lax.dynamic_index_in_dim(local_valid, outer_index, 0, keepdims=False)
    slotted = select_rows(slot_source, slot_valid, group_sum)
    owned = summed_on_arrival(slotted, "gy", 0)
    return (hidden_grad, owned.reshape(1, 1, most, 128))


def solution(mesh):
    placed = (
        P(("gx", "gy"), "gz"),
        P("gz"),
        P(("gx", "gy"), "gz"),
        P(("gx", "gy"), None),
        P(("gx", "gy"), "gz", None, None),
        P("gz", None),
    )
    return jax.shard_map(
        shards,
        mesh=mesh,
        in_specs=placed,
        out_specs=(P(("gx", "gy"), "gz"), P(("gx", "gy"), "gz", None, None)),
        check_vma=False,
    )
```

profile of v0, /device:TPU:1, one launch (start us, length us, event | category | flops | bytes accessed | tf_op | source)
XLA Modules:
  0.0 479.5 jit_solution(13150978717548217782)
XLA Ops:
  10.6 207.6 %while.35 = (s32[]{:T(128)}, u32[4096]{0:T(1024)S(1)}, u32[4096]{0:T(1024)S(1)}, s32[192]{0:T(256)S(1)}, s32[]{:T(128)}, /*index=5*/s32[]{:T(128)}, s32[]{}) while((s32[]{:T(128)}, u32[4096]{0:T(1024)S(1)}, u32[4096]{0:T(1024)S(1)}, s32[192]{0:T(256)S(1)}, s32[]{:T(128)}, /*index=5*/s32[]{:T(128)}, s32[]{}) %tuple.60), condition=%wide.region_3.4_spmd.clone, body=%wide.region_2.3_spmd.clone.sunk | while | flops 77828 | bytes 254053 | solution.py:36
  10.6 25.9 %gather_fusion = s32[4096]{0:T(1024)S(1)} fusion(s32[192]{0:T(256)S(1)} %get-tuple-element.216, u32[4096]{0:T(1024)S(1)} %broadcast_clamp_fusion.2), kind=kCustom, calls=%fused_computation.clone.clone.1 | custom fusion | bytes 49152 | tf_op jit(solution)/shard_map/jit(searchsorted)/jit(_searchsorted_scan_impl)/vmap(jit(_searchsorted_scan_impl))/while/body/eval_jaxpr/gather | solution.py:36
  36.6 25.9 %gather_fusion = s32[4096]{0:T(1024)S(1)} fusion(s32[192]{0:T(256)S(1)} %get-tuple-element.216, u32[4096]{0:T(1024)S(1)} %broadcast_clamp_fusion.2), kind=kCustom, calls=%fused_computation.clone.clone.1 | custom fusion | bytes 49152 | tf_op jit(solution)/shard_map/jit(searchsorted)/jit(_searchsorted_scan_impl)/vmap(jit(_searchsorted_scan_impl))/while/body/eval_jaxpr/gather | solution.py:36
  62.5 25.9 %gather_fusion = s32[4096]{0:T(1024)S(1)} fusion(s32[192]{0:T(256)S(1)} %get-tuple-element.216, u32[4096]{0:T(1024)S(1)} %broadcast_clamp_fusion.2), kind=kCustom, calls=%fused_computation.clone.clone.1 | custom fusion | bytes 49152 | tf_op jit(solution)/shard_map/jit(searchsorted)/jit(_searchsorted_scan_impl)/vmap(jit(_searchsorted_scan_impl))/while/body/eval_jaxpr/gather | solution.py:36
  88.5 25.9 %gather_fusion = s32[4096]{0:T(1024)S(1)} fusion(s32[192]{0:T(256)S(1)} %get-tuple-element.216, u32[4096]{0:T(1024)S(1)} %broadcast_clamp_fusion.2), kind=kCustom, calls=%fused_computation.clone.clone.1 | custom fusion | bytes 49152 | tf_op jit(solution)/shard_map/jit(searchsorted)/jit(_searchsorted_scan_impl)/vmap(jit(_searchsorted_scan_impl))/while/body/eval_jaxpr/gather | solution.py:36
  114.4 25.9 %gather_fusion = s32[4096]{0:T(1024)S(1)} fusion(s32[192]{0:T(256)S(1)} %get-tuple-element.216, u32[4096]{0:T(1024)S(1)} %broadcast_clamp_fusion.2), kind=kCustom, calls=%fused_computation.clone.clone.1 | custom fusion | bytes 49152 | tf_op jit(solution)/shard_map/jit(searchsorted)/jit(_searchsorted_scan_impl)/vmap(jit(_searchsorted_scan_impl))/while/body/eval_jaxpr/gather | solution.py:36
  140.4 25.9 %gather_fusion = s32[4096]{0:T(1024)S(1)} fusion(s32[192]{0:T(256)S(1)} %get-tuple-element.216, u32[4096]{0:T(1024)S(1)} %broadcast_clamp_fusion.2), kind=kCustom, calls=%fused_computation.clone.clone.1 | custom fusion | bytes 49152 | tf_op jit(solution)/shard_map/jit(searchsorted)/jit(_searchsorted_scan_impl)/vmap(jit(_searchsorted_scan_impl))/while/body/eval_jaxpr/gather | solution.py:36
  166.3 25.9 %gather_fusion = s32[4096]{0:T(1024)S(1)} fusion(s32[192]{0:T(256)S(1)} %get-tuple-element.216, u32[4096]{0:T(1024)S(1)} %broadcast_clamp_fusion.2), kind=kCustom, calls=%fused_computation.clone.clone.1 | custom fusion | bytes 49152 | tf_op jit(solution)/shard_map/jit(searchsorted)/jit(_searchsorted_scan_impl)/vmap(jit(_searchsorted_scan_impl))/while/body/eval_jaxpr/gather | solution.py:36
  192.3 25.9 %gather_fusion = s32[4096]{0:T(1024)S(1)} fusion(s32[192]{0:T(256)S(1)} %get-tuple-element.216, u32[4096]{0:T(1024)S(1)} %broadcast_clamp_fusion.2), kind=kCustom, calls=%fused_computation.clone.clone.1 | custom fusion | bytes 49152 | tf_op jit(solution)/shard_map/jit(searchsorted)/jit(_searchsorted_scan_impl)/vmap(jit(_searchsorted_scan_impl))/while/body/eval_jaxpr/gather | solution.py:36
  218.3 25.9 %gather_fusion.1 = s32[4096]{0:T(1024)S(1)} fusion(s32[192]{0:T(256)S(1)} %get-tuple-element.141, s32[4096]{0:T(1024)S(1)} %fusion.30), kind=kCustom, calls=%fused_computation.1 | custom fusion | bytes 49152 | tf_op jit(solution)/shard_map/gather | solution.py:37
  245.8 95.8 %all-gather.3.cloned.1.call-done = bf16[1,1,5568,128]{3,1,0,2:T(2,128)(2,1)} async-done(((bf16[1,1,29,128]{3,1,0,2:T(2,128)(2,1)}), bf16[1,1,5568,128]{3,1,0,2:T(2,128)(2,1)}) %all-gather.3.cloned.1.call-update) | async-done | bytes 1425424 | tf_op jit(solution)/shard_map/all_gather | solution.py:95
  341.6 2.0 copy.32
  343.6 4.5 while.34
  349.6 12.8 %all_to_all.22 = f32[4,1,128]{2,1,0:T(1,128)S(1)} all-to-all(f32[4,1,128]{2,1,0:T(1,128)S(1)} %broadcast_in_dim.63), channel_id=1, replica_groups=mesh['gx'=12,'gy'=16,'gz'=4] {'gz'}, dimensions={0} | all-to-all | bytes 4096 | tf_op jit(solution)/shard_map/all_to_all | solution.py:11
  363.0 3.2 all-to-all-start
  366.2 6.4 %all-to-all-done = f32[4,1,128]{2,1,0:T(1,128)S(1)} async-done(((f32[4,1,128]{2,1,0:T(1,128)}), f32[4,1,128]{2,1,0:T(1,128)S(1)}, u32[]{:S(2)}, u32[]{:S(2)}) %all-to-all-start) | async-done | bytes 2080 | tf_op jit(solution)/shard_map/all_to_all | solution.py:11
  373.2 1.4 reshape.158
  374.6 1.7 pad.9
  376.3 1.5 reshape.159
  377.8 6.3 %all-to-all-start.2 = ((f32[12,342,128]{2,1,0:T(8,128)}), f32[12,342,128]{2,1,0:T(8,128)S(1)}, u32[]{:S(2)}, u32[]{:S(2)}) async-start(f32[12,342,128]{2,1,0:T(8,128)} %reshape.159), calls=%async_computation.2 | async-start | bytes 4227072 | tf_op jit(solution)/shard_map/all_to_all | solution.py:28
  384.3 32.9 %gather_fusion.2 = s32[5568]{0:T(1024)S(1)} fusion(s32[192]{0:T(256)S(1)} %get-tuple-element.141, s32[6144]{0:T(1024)S(1)} %pad_clamp_fusion), kind=kCustom, calls=%fused_computation.2 | custom fusion | bytes 66816 | tf_op jit(solution)/shard_map/gather | solution.py:41
  417.3 32.9 %gather_fusion.3 = s32[5568]{0:T(1024)S(1)} fusion(s32[192]{0:T(256)S(1)} %bitcast.34, s32[6144]{0:T(1024)S(1)} %pad_clamp_fusion), kind=kCustom, calls=%fused_computation.3 | custom fusion | bytes 66816 | tf_op jit(solution)/shard_map/gather | solution.py:40
  453.3 11.5 %all-to-all-start.3 = ((f32[16,29,128]{2,1,0:T(8,128)}), f32[16,29,128]{2,1,0:T(8,128)S(1)}, u32[]{:S(2)}, u32[]{:S(2)}) async-start(f32[16,29,128]{2,1,0:T(8,128)} %fusion.11), calls=%async_computation.3 | async-start | bytes 524288 | tf_op jit(solution)/shard_map/all_to_all | solution.py:28
  465.8 6.2 %all-to-all-done.3 = f32[16,29,128]{2,1,0:T(8,128)S(1)} async-done(((f32[16,29,128]{2,1,0:T(8,128)}), f32[16,29,128]{2,1,0:T(8,128)S(1)}, u32[]{:S(2)}, u32[]{:S(2)}) %all-to-all-start.3) | async-done | bytes 237600 | tf_op jit(solution)/shard_map/all_to_all | solution.py:28
  (116 shorter events, 17.0 us)
Async XLA Ops:
  7.2 342.0 %copy-start = (bf16[128,512]{1,0:T(8,128)(2,1)S(1)}, bf16[128,512]{1,0:T(8,128)(2,1)}, u32[]{:S(2)}) copy-start(bf16[128,512]{1,0:T(8,128)(2,1)} %param.13) | copy-start | bytes 393220
  7.2 334.4 %all-gather.3.cloned.1.call-start = ((), (), s32[]{:S(2)}) async-start(), calls=%async_computation.4 | async-start | bytes 2865664 | tf_op jit(solution)/shard_map/all_gather | solution.py:95
  218.3 27.1 %copy-start.2 = (bf16[128,1024]{1,0:T(8,128)(2,1)S(1)}, bf16[128,1024]{1,0:T(8,128)(2,1)}, u32[]{:S(2)}) copy-start(bf16[128,1024]{1,0:T(8,128)(2,1)} %param.10) | copy-start | bytes 786436
  218.3 27.3 %copy-start.3 = (bf16[128,1024]{1,0:T(8,128)(2,1)S(1)}, bf16[128,1024]{1,0:T(8,128)(2,1)}, u32[]{:S(2)}) copy-start(bf16[128,1024]{1,0:T(8,128)(2,1)} %param.12) | copy-start | bytes 786436
  348.4 0.7 copy-start.4
  363.0 9.7 %all-to-all-start = ((f32[4,1,128]{2,1,0:T(1,128)}), f32[4,1,128]{2,1,0:T(1,128)S(1)}, u32[]{:S(2)}, u32[]{:S(2)}) async-start(f32[4,1,128]{2,1,0:T(1,128)} %broadcast_in_dim.62), calls=%async_computation | async-start | bytes 4096 | tf_op jit(solution)/shard_map/all_to_all | solution.py:11
  377.8 74.1 %all-to-all-start.2 = ((f32[12,342,128]{2,1,0:T(8,128)}), f32[12,342,128]{2,1,0:T(8,128)S(1)}, u32[]{:S(2)}, u32[]{:S(2)}) async-start(f32[12,342,128]{2,1,0:T(8,128)} %reshape.159), calls=%async_computation.2 | async-start | bytes 4227072 | tf_op jit(solution)/shard_map/all_to_all | solution.py:28
  384.3 33.0 %copy-start.1 = (s32[1,192]{1,0:T(1,128)S(1)}, s32[1,192]{1,0:T(1,128)}, u32[]{:S(2)}) copy-start(s32[1,192]{1,0:T(1,128)} %param.15) | copy-start | bytes 2308
  453.3 18.7 %all-to-all-start.3 = ((f32[16,29,128]{2,1,0:T(8,128)}), f32[16,29,128]{2,1,0:T(8,128)S(1)}, u32[]{:S(2)}, u32[]{:S(2)}) async-start(f32[16,29,128]{2,1,0:T(8,128)} %fusion.11), calls=%async_computation.3 | async-start | bytes 524288 | tf_op jit(solution)/shard_map/all_to_all | solution.py:28
Sparse Core Ops, SparseCore 0:
  11.1 330.4 all-gather.2
where the time goes:
time: 480 us
  local copies, waits for them, and re-layouts  313 us (65%)
  waiting for transfers between devices  108 us (22%)
  starting transfers between devices  21.1 us (4%)
  between operations  14.4 us (3%)
  blocking collectives  12.8 us (3%)
  matrix products  6.17 us (1%)
    gather x8, local copies, waits for them, and re-layouts, block_layout(): owner = jnp.searchsorted(ends, block_ids, side='right')  207 us
    all_gather x1, waiting for transfers between devices, shards(): gathered = lax.all_gather(local_blocks, ('gx', 'gy'), axis=0, tiled=True)  95.8 us
    gather x2, local copies, waits for them, and re-layouts, block_layout(): source = jnp.clip(starts[slot_owner] + slot_within, 0, blocks - 1)  33 us
    gather x2, local copies, waits for them, and re-layouts, block_layout(): valid = slot_within < counts[slot_owner]  33 us
    gather x1, local copies, waits for them, and re-layouts, block_layout(): gather_index = owner * most + block_ids - starts[owner]  25.9 us
    all_to_all x2, starting transfers between devices, summed_on_arrival(): lax.all_to_all(blocks, axis, split_axis=0, concat_axis=0, tiled=True)  17.8 us
    all_to_all x1, blocking collectives, sent_to_all(): lax.all_to_all(jnp.broadcast_to(shard[None], (count, *shard.shape)), axis...  12.8 us
  transfers between devices with their start and end apart: 4, of which 3 were waited for; matrix products, arithmetic and copies ran while one was open for 64% of the time, Pallas kernels for 0%

commit v1 on v0

v1 whole, which is shorter than its diff:
```python
import functools

import jax
import jax.numpy as jnp
from jax import lax
from jax.experimental import pallas as pl
from jax.experimental.pallas import tpu as pltpu
from jax.sharding import PartitionSpec as P

EPS = 1e-06
LANES = 128
CORES = 2
F32 = jnp.float32
BF16 = jnp.bfloat16
MESH = pl.DeviceIdType.MESH
BATCHES = 4


def round_up(value, step):
    return (value + step - 1) // step * step


def iota(shape, dim):
    return lax.broadcasted_iota(jnp.int32, shape, dim)


def nt_dot(a, b):
    return lax.dot_general(a, b, (((1,), (1,)), ((), ())), preferred_element_type=F32)


def as_column(row):
    return jnp.transpose(jnp.broadcast_to(row, (LANES, LANES)))


def lane_groups(rows):
    return [slice(g * LANES, (g + 1) * LANES) for g in range(rows // LANES)]


def kernel(
    cfg,
    h_hbm, gain_hbm, ng_hbm, kg_hbm, wb_hbm, cnt_hbm,
    hg_hbm, wg_ref,
    h2, gainv, ngv, kg2, wbv, cntv,
    sq, pj, rs, nrm, onehot, onehot_t, jcol,
    gathered, send, recv, zsend, zrecv, wfull, p_own, p_send, p_recv, hgv,
    local_sem, sq_s, sq_r, sib_s, sib_r, c1_s, c1_r, b_s, b_r, c2_s, c2_r, pj_s, pj_r, z_s, z_r,
):
    outer, inner, quarters, chips = cfg["outer"], cfg["inner"], cfg["quarters"], cfg["chips"]
    slots, most, group_blocks, blocks = cfg["slots"], cfg["most"], cfg["group_blocks"], cfg["blocks"]
    rows, width, pieces, model_width = cfg["rows"], cfg["width"], cfg["pieces"], cfg["model_width"]
    lane_window, row_window, padded_outer = cfg["lane_window"], cfg["row_window"], cfg["padded_outer"]
    per_group = chips * slots
    owners = outer * inner
    slot_bits = slots.bit_length() - 1
    inner_bits = inner.bit_length() - 1
    piece_bits = pieces.bit_length() - 1

    x = lax.axis_index("gx")
    y = lax.axis_index("gy")
    q = lax.axis_index("gz")
    core = lax.rem(y, CORES)
    chip = y // CORES
    other = 1 - core
    own_rows = pl.ds(pl.multiple_of(core * LANES, LANES), LANES)
    other_rows = pl.ds(pl.multiple_of(other * LANES, LANES), LANES)

    def at(gx, gchip, gcore, gz):
        return (gx, gchip * CORES + gcore, gz)

    z_peers = [(k, lax.rem(x + k, outer)) for k in range(1, outer)]
    z_peers.sort(key=lambda p: -min(p[0], outer - p[0]))
    chip_peers = [(k, lax.rem(chip + k, chips)) for k in range(1, chips)]
    gz_peers = [
        (dc * quarters + dq - 1, lax.rem(core + dc, CORES), lax.rem(q + dq, quarters))
        for dc in range(CORES)
        for dq in range(quarters)
        if dc or dq
    ]

    loads = [
        pltpu.make_async_copy(h_hbm, h2.at[core], local_sem.at[0]),
        pltpu.make_async_copy(cnt_hbm, cntv, local_sem.at[1]),
        pltpu.make_async_copy(wb_hbm, wbv, local_sem.at[2]),
        pltpu.make_async_copy(kg_hbm, kg2.at[own_rows], local_sem.at[3]),
        pltpu.make_async_copy(gain_hbm, gainv, local_sem.at[4]),
        pltpu.make_async_copy(ng_hbm, ngv, local_sem.at[5]),
    ]
    for copy in loads:
        copy.start()
    barrier = pltpu.get_barrier_semaphore()
    peers = [at(zx, chip, core, q) for _, zx in z_peers]
    peers += [at(x, other_chip, core, q) for _, other_chip in chip_peers]
    peers += [at(x, chip, gcore, gq) for _, gcore, gq in gz_peers]
    for peer in peers:
        pl.semaphore_signal(barrier, inc=1, device_id=peer, device_id_type=MESH)

    groups = lane_groups(rows)

    loads[0].wait()
    partial = jnp.zeros((LANES, LANES), F32)
    for g in groups:
        piece = h2[core, :, g].astype(F32)
        partial = partial + piece * piece
    row = jnp.sum(jnp.transpose(partial), axis=0, keepdims=True)
    sq[core, q] = jnp.broadcast_to(row, (8, LANES))

    loads[2].wait()
    own_blocks = jnp.concatenate(
        [wbv[0, 0].astype(F32), jnp.zeros((slots - most, LANES), F32)], axis=0
    )
    gathered[chip, x] = own_blocks.astype(BF16)
    loads[3].wait()

    pl.semaphore_wait(barrier, len(peers))

    sends = []

    def push(src, dst, send_sem, recv_sem, peer):
        copy = pltpu.make_async_remote_copy(
            src_ref=src, dst_ref=dst, send_sem=send_sem, recv_sem=recv_sem,
            device_id=peer, device_id_type=MESH,
        )
        copy.start()
        sends.append(copy)
        return copy

    sq_copies = [
        push(sq.at[core, q], sq.at[core, q], sq_s.at[m], sq_r.at[m], at(x, chip, gcore, gq))
        for m, gcore, gq in gz_peers
    ]
    c1_copies = [
        push(gathered.at[chip, x], gathered.at[chip, x], c1_s.at[k - 1], c1_r.at[k - 1], at(zx, chip, core, q))
        for k, zx in z_peers
    ]
    sibling = at(x, chip, other, q)
    sib_copies = [
        push(kg2.at[own_rows], kg2.at[own_rows], sib_s.at[0], sib_r.at[0], sibling),
        push(h2.at[core], h2.at[core], sib_s.at[1], sib_r.at[1], sibling),
    ]

    loads[1].wait()
    loads[4].wait()
    counts = cntv[...].astype(F32)
    owner_of = iota((padded_outer, owners), 1)
    of_group = (owner_of >> inner_bits) == iota((padded_outer, owners), 0)
    by_group = jnp.where(of_group, jnp.broadcast_to(counts, (padded_outer, owners)), 0.0).astype(BF16)

    def placed(shape, slot_dim, owner_dim):
        slot = iota(shape, slot_dim)
        holder = (slot >> slot_bits) * CORES + core
        within = iota(shape, owner_dim) & (inner - 1)
        before = jnp.where(within < holder, 1.0, 0.0).astype(BF16)
        mine = jnp.where(within == holder, 1.0, 0.0).astype(BF16)
        return before, mine

    before, mine = placed((per_group, owners), 0, 1)
    start_c = nt_dot(before, by_group).astype(jnp.int32)
    count_c = nt_dot(mine, by_group).astype(jnp.int32)
    within_c = iota((per_group, padded_outer), 0) & (slots - 1)
    block_c = start_c + within_c + group_blocks * iota((per_group, padded_outer), 1)
    block_c = jnp.where(within_c < count_c, block_c, -pieces)
    row_c = block_c >> piece_bits
    jcol[...] = block_c & (pieces - 1)
    start_r = nt_dot(by_group, before).astype(jnp.int32)
    count_r = nt_dot(by_group, mine).astype(jnp.int32)
    within_r = iota((padded_outer, per_group), 1) & (slots - 1)
    block_r = start_r + within_r + group_blocks * iota((padded_outer, per_group), 0)
    block_r = jnp.where(within_r < count_r, block_r, -pieces)
    row_r = block_r >> piece_bits

    def windows(z):
        first = group_blocks * z // pieces
        return (
            min(first // LANES * LANES, rows - lane_window),
            min(first // 8 * 8, rows - row_window),
        )

    for z in range(outer):
        lane0, row0 = windows(z)
        hit = row_c[:, z : z + 1] == lane0 + iota((per_group, lane_window), 1)
        onehot[z] = jnp.where(hit, 1.0, 0.0).astype(BF16)
        hit = row_r[z : z + 1, :] == row0 + iota((row_window, per_group), 0)
        onehot_t[z] = jnp.where(hit, 1.0, 0.0).astype(BF16)
    wfull[...] = jnp.zeros_like(wfull)

    for copy in sq_copies:
        copy.wait_recv()
    for copy in sib_copies:
        copy.wait_recv()
    for c in range(CORES):
        total = sq[c, 0, 0:1]
        for other_q in range(1, quarters):
            total = total + sq[c, other_q, 0:1]
        rs[c] = as_column(lax.rsqrt(total / model_width + EPS))
        for g in groups:
            scaled = h2[c, :, g].astype(F32) * rs[c] * gainv[:, g]
            nrm[c * LANES : (c + 1) * LANES, g] = scaled.astype(BF16)

    step = outer // BATCHES
    b_copies = []
    for batch in range(BATCHES):
        for z in range(batch * step, (batch + 1) * step):
            lane0, _ = windows(z)
            picked = nt_dot(onehot[z], nrm[:, lane0 : lane0 + lane_window]).astype(BF16)
            product = jnp.dot(picked, kg2[...], preferred_element_type=F32)
            piece_of = jcol[:, z : z + 1]
            value = product[:, :LANES]
            for j in range(1, pieces):
                value = jnp.where(piece_of == j, product[:, j * LANES : (j + 1) * LANES], value)
            send[:, z] = value.astype(BF16).reshape(chips, slots, LANES)
        span = pl.ds(batch * step, step)
        b_copies.append([
            push(
                send.at[to, span], recv.at[k - 1, span], b_s.at[k - 1, batch], b_r.at[k - 1, batch],
                at(x, to, core, q),
            )
            for k, to in chip_peers
        ])

    for copy in c1_copies:
        copy.wait_recv()
    c2_copies = [
        push(gathered.at[chip], gathered.at[chip], c2_s.at[k - 1], c2_r.at[k - 1], at(x, to, core, q))
        for k, to in chip_peers
    ]

    for batch in range(BATCHES):
        for copy in b_copies[batch]:
            copy.wait_recv()
        for z in range(batch * step, (batch + 1) * step):
            total = send[chip, z].astype(F32)
            for k in range(1, chips):
                total = total + recv[k - 1, z].astype(F32)
            zsend[z] = total
    zz_copies = [
        push(zsend.at[zx], zrecv.at[k - 1], z_s.at[k - 1], z_r.at[k - 1], at(zx, chip, core, q))
        for k, zx in z_peers
    ]

    for copy in c2_copies:
        copy.wait_recv()
    for z in range(outer):
        _, row0 = windows(z)
        values = gathered[:, z].reshape(per_group, LANES)
        piece_of = jcol[:, z : z + 1]
        spread = jnp.concatenate(
            [jnp.where(piece_of == j, values, jnp.zeros_like(values)) for j in range(pieces)], axis=1
        )
        wfull[row0 : row0 + row_window, :] += jnp.dot(
            onehot_t[z], spread, preferred_element_type=F32
        )
    weight = wfull[...].astype(BF16)
    p_send[...] = nt_dot(kg2[other_rows], weight)
    p_copy = push(p_send, p_recv, sib_s.at[2], sib_r.at[2], sibling)
    p_own[...] = nt_dot(kg2[own_rows], weight)

    loads[5].wait()
    p_copy.wait_recv()
    partial = jnp.zeros((LANES, LANES), F32)
    for g in groups:
        dnorm = ngv[:, g].astype(F32) + (p_own[:, g] + p_recv[:, g])
        gained = gainv[:, g] * dnorm
        p_own[:, g] = gained
        partial = partial + gained * h2[core, :, g].astype(F32)
    row = jnp.sum(jnp.transpose(partial), axis=0, keepdims=True)
    pj[q] = jnp.broadcast_to(row, (8, LANES))
    pj_copies = [
        push(pj.at[q], pj.at[q], pj_s.at[dq - 1], pj_r.at[dq - 1], at(x, chip, core, lax.rem(q + dq, quarters)))
        for dq in range(1, quarters)
    ]
    for copy in pj_copies:
        copy.wait_recv()
    proj = pj[0, 0:1]
    for other_q in range(1, quarters):
        proj = proj + pj[other_q, 0:1]
    rstd = rs[core]
    coefficient = rstd * rstd * rstd * as_column(proj) / model_width
    for g in groups:
        grad = p_own[:, g] * rstd - h2[core, :, g].astype(F32) * coefficient
        hgv[:, g] = grad.astype(BF16)
    store = pltpu.make_async_copy(hgv, hg_hbm, local_sem.at[6])
    store.start()

    for copy in zz_copies:
        copy.wait_recv()
    total = zsend[x]
    for k in range(1, outer):
        total = total + zrecv[k - 1]
    wg_ref[0, 0] = total[:most]
    store.wait()
    for copy in sends:
        copy.wait_send()


def shards(hidden_in, norm_gain, normed_grad, key_grad, weight_blocks, block_count):
    outer, inner, quarters = lax.axis_size("gx"), lax.axis_size("gy"), lax.axis_size("gz")
    tokens, rows = hidden_in.shape
    width = key_grad.shape[1]
    most = weight_blocks.shape[2]
    blocks = rows * width // LANES
    pieces = width // LANES
    group_blocks = (blocks + outer - 1) // outer
    slots = round_up(most, 32)
    chips = inner // CORES
    per_group = chips * slots
    padded_outer = round_up(outer, 16)
    span = (group_blocks + pieces - 1) // pieces + 1
    cfg = dict(
        outer=outer, inner=inner, quarters=quarters, chips=chips, slots=slots, most=most,
        group_blocks=group_blocks, blocks=blocks, rows=rows, width=width, pieces=pieces,
        model_width=rows * quarters, padded_outer=padded_outer,
        lane_window=min(rows, round_up(span + LANES - 1, LANES)),
        row_window=min(rows, round_up(span + 7, 8)),
    )
    vmem = pltpu.VMEM
    dma = pltpu.SemaphoreType.DMA
    hg, wg = pl.pallas_call(
        functools.partial(kernel, cfg),
        out_shape=(
            jax.ShapeDtypeStruct((tokens, rows), BF16),
            jax.ShapeDtypeStruct(weight_blocks.shape, F32),
        ),
        in_specs=[pl.BlockSpec(memory_space=pl.ANY)] * 6,
        out_specs=(pl.BlockSpec(memory_space=pl.ANY), pl.BlockSpec(memory_space=pltpu.VMEM)),
        scratch_shapes=[
            vmem((CORES, tokens, rows), BF16),
            vmem((1, rows), F32),
            vmem((tokens, rows), BF16),
            vmem((CORES * tokens, width), BF16),
            vmem(weight_blocks.shape, BF16),
            vmem(block_count.shape, jnp.int32),
            vmem((CORES, quarters, 8, LANES), F32),
            vmem((quarters, 8, LANES), F32),
            vmem((CORES, LANES, LANES), F32),
            vmem((CORES * tokens, rows), BF16),
            vmem((outer, per_group, cfg["lane_window"]), BF16),
            vmem((outer, cfg["row_window"], per_group), BF16),
            vmem((per_group, padded_outer), jnp.int32),
            vmem((chips, outer, slots, LANES), BF16),
            vmem((chips, outer, slots, LANES), BF16),
            vmem((chips - 1, outer, slots, LANES), BF16),
            vmem((outer, slots, LANES), F32),
            vmem((outer - 1, slots, LANES), F32),
            vmem((rows, width), F32),
            vmem((tokens, rows), F32),
            vmem((tokens, rows), F32),
            vmem((tokens, rows), F32),
            vmem((tokens, rows), BF16),
            dma((7,)),
            dma((CORES * quarters - 1,)), dma((CORES * quarters - 1,)),
            dma((3,)), dma((3,)),
            dma((outer - 1,)), dma((outer - 1,)),
            dma((chips - 1, BATCHES)), dma((chips - 1, BATCHES)),
            dma((chips - 1,)), dma((chips - 1,)),
            dma((quarters - 1,)), dma((quarters - 1,)),
            dma((outer - 1,)), dma((outer - 1,)),
        ],
        compiler_params=pltpu.CompilerParams(
            collective_id=0, has_side_effects=True, vmem_limit_bytes=48 * 1024 * 1024
        ),
        name="key_projection_backward",
    )(hidden_in, norm_gain.reshape(1, rows), normed_grad, key_grad, weight_blocks, block_count)
    return hg, wg


def solution(mesh):
    placed = (
        P(("gx", "gy"), "gz"),
        P("gz"),
        P(("gx", "gy"), "gz"),
        P(("gx", "gy"), None),
        P(("gx", "gy"), "gz", None, None),
        P("gz", None),
    )
    return jax.shard_map(
        shards,
        mesh=mesh,
        in_specs=placed,
        out_specs=(P(("gx", "gy"), "gz"), P(("gx", "gy"), "gz", None, None)),
        check_vma=False,
    )
```

time: 480 us -> 60.6 us (0.13)
  local copies, waits for them, and re-layouts: 313 us -> 6.18 us
  waiting for transfers between devices: 108 us -> 0 us
  Pallas kernels: 0 us -> 53.5 us
  starting transfers between devices: 21.1 us -> 0 us
  between operations: 14.4 us -> 0.65 us
  blocking collectives: 12.8 us -> 0 us
  matrix products: 6.17 us -> 0 us
    gather x13 -> x0, local copies, waits for them, and re-layouts: 299 us -> none  [the longest x8 207 us: block_layout(): owner = jnp.searchsorted(ends, block_ids, side='right')]
    all_gather x1 -> x0, waiting for transfers between devices: 95.8 us -> none  [shards(): gathered = lax.all_gather(local_blocks, ('gx', 'gy'), axis=0, tiled=True)]
    pallas_call x0 -> x1, Pallas kernels: none -> 53.5 us  [shards(): pl.pallas_call(functools.partial(kernel, cfg), out_shape=(jax.ShapeDtypeS...]
    all_to_all x3 -> x0, starting transfers between devices: 21 us -> none  [the longest x2 17.8 us: summed_on_arrival(): lax.all_to_all(blocks, axis, split_axis=0, concat_axis=0, tiled=True)]
    all_to_all x1 -> x0, blocking collectives: 12.8 us -> none  [sent_to_all(): lax.all_to_all(jnp.broadcast_to(shard[None], (count, *shard.shape)), axis...]
    all_to_all x3 -> x0, waiting for transfers between devices: 12.7 us -> none  [the longest x1 6.41 us: sent_to_all(): lax.all_to_all(jnp.broadcast_to(shard[None], (count, *shard.shape)), axis...]
    dot_general x15 -> x0, matrix products: 6.17 us -> none  [the longest x12 3.96 us: select_rows(): jnp.dot(onehot.astype(jnp.bfloat16), rows, preferred_element_type=jnp.flo...]
  transfers between devices with their start and end apart: 4 -> 0, of which waited for: 3 -> 0; matrix products, arithmetic and copies ran while one was open for 64% -> 0% of each run, Pallas kernels for 0% -> 0%
where the time goes in v1:
time: 60.6 us; the launch traced here: 60.3 us
  Pallas kernels  53.5 us (88%)
  local copies, waits for them, and re-layouts  6.18 us (10%)
  between operations  0.65 us (1%)
    pallas_call x1, Pallas kernels, shards(): pl.pallas_call(functools.partial(kernel, cfg), out_shape=(jax.ShapeDtypeS...  53.5 us
    unnamed x13, local copies, waits for them, and re-layouts  5.56 us

profile of v1, /device:TPU:1, one launch (start us, length us, event | category | flops | bytes accessed | tf_op | source)
XLA Modules:
  0.0 60.3 jit_solution(6384299201793214771)
XLA Ops:
  0.6 0.0 copy-start.5
  0.6 0.7 %copy-done.5 = s32[1,192]{1,0:T(1,128)S(1)} copy-done((s32[1,192]{1,0:T(1,128)S(1)}, s32[1,192]{1,0:T(1,128)}, u32[]{:S(2)}) %copy-start.5) | copy-done | bytes 792
  1.3 0.0 copy-start
  1.3 0.9 %copy-done = bf16[128,1024]{1,0:T(8,128)(2,1)S(1)} copy-done((bf16[128,1024]{1,0:T(8,128)(2,1)S(1)}, bf16[128,1024]{1,0:T(8,128)(2,1)}, u32[]{:S(2)}) %copy-start) | copy-done | bytes 262168
  2.3 0.0 copy-start.1
  2.3 0.9 %copy-done.1 = bf16[128,1024]{1,0:T(8,128)(2,1)S(1)} copy-done((bf16[128,1024]{1,0:T(8,128)(2,1)S(1)}, bf16[128,1024]{1,0:T(8,128)(2,1)}, u32[]{:S(2)}) %copy-start.1) | copy-done | bytes 262168
  3.2 0.0 copy-start.2
  3.2 0.9 %copy-done.2 = bf16[128,512]{1,0:T(8,128)(2,1)S(1)} copy-done((bf16[128,512]{1,0:T(8,128)(2,1)S(1)}, bf16[128,512]{1,0:T(8,128)(2,1)}, u32[]{:S(2)}) %copy-start.2) | copy-done | bytes 131096
  4.1 0.0 copy-start.3
  4.1 0.7 %copy-done.3 = bf16[1,1,29,128]{3,2,1,0:T(8,128)(2,1)S(1)} copy-done((bf16[1,1,29,128]{3,2,1,0:T(8,128)(2,1)S(1)}, bf16[1,1,29,128]{3,2,1,0:T(8,128)(2,1)}, u32[]{:S(2)}) %copy-start.3) | copy-done | bytes 7448
  4.8 0.0 copy-start.4
  4.8 0.7 %copy-done.4 = f32[1024]{0:T(1024)S(1)} copy-done((f32[1024]{0:T(1024)S(1)}, f32[1024]{0:T(1024)}, u32[]{:S(2)}) %copy-start.4) | copy-done | bytes 4120
  5.5 53.5 %key_projection_backward.1 = (bf16[128,1024]{1,0:T(8,128)(2,1)S(1)}, f32[1,1,29,128]{3,2,1,0:T(8,128)S(1)}) custom-call(bf16[128,1024]{1,0:T(8,128)(2,1)S(1)} %copy-done, f32[1,1024]{1,0:T(1,128)S(1)} %bitcast.1, bf16[128,1024]{1,0:T(8,128)(2,1)S(1)} %copy-done.1, bf16[128,512]{1,0:T(8,128)(2,1)S(1)} %copy-done.2, bf16[1,1,29,128]{3,2,1,0:T(8,128)(2,1)S(1)} %copy-done.3, ...), custom_call_target="tpu_custom_call" | custom-call | tf_op jit(solution)/shard_map/key_projection_backward/pallas_call | solution.py:317
  59.0 0.6 %copy.8 = f32[1,1,29,128]{3,1,2,0:T(1,128)} copy(f32[1,1,29,128]{3,2,1,0:T(8,128)S(1)} %get-tuple-element.3) | data formatting | bytes 29696 | tf_op jit(solution)/shard_map/key_projection_backward/pallas_call | solution.py:317
  59.6 0.7 %copy.10 = bf16[128,1024]{1,0:T(8,128)(2,1)} copy(bf16[128,1024]{1,0:T(8,128)(2,1)S(1)} %get-tuple-element.6) | data formatting | bytes 524288
Async XLA Ops:
  0.6 0.7 %copy-start.5 = (s32[1,192]{1,0:T(1,128)S(1)}, s32[1,192]{1,0:T(1,128)}, u32[]{:S(2)}) copy-start(s32[1,192]{1,0:T(1,128)} %cnt_hbm.1) | copy-start | bytes 2308
  1.3 0.9 %copy-start = (bf16[128,1024]{1,0:T(8,128)(2,1)S(1)}, bf16[128,1024]{1,0:T(8,128)(2,1)}, u32[]{:S(2)}) copy-start(bf16[128,1024]{1,0:T(8,128)(2,1)} %h_hbm.1) | copy-start | bytes 786436
  2.3 0.9 %copy-start.1 = (bf16[128,1024]{1,0:T(8,128)(2,1)S(1)}, bf16[128,1024]{1,0:T(8,128)(2,1)}, u32[]{:S(2)}) copy-start(bf16[128,1024]{1,0:T(8,128)(2,1)} %ng_hbm.1) | copy-start | bytes 786436
  3.2 0.9 %copy-start.2 = (bf16[128,512]{1,0:T(8,128)(2,1)S(1)}, bf16[128,512]{1,0:T(8,128)(2,1)}, u32[]{:S(2)}) copy-start(bf16[128,512]{1,0:T(8,128)(2,1)} %kg_hbm.1) | copy-start | bytes 393220
  4.1 0.7 %copy-start.3 = (bf16[1,1,29,128]{3,2,1,0:T(8,128)(2,1)S(1)}, bf16[1,1,29,128]{3,2,1,0:T(8,128)(2,1)}, u32[]{:S(2)}) copy-start(bf16[1,1,29,128]{3,2,1,0:T(8,128)(2,1)} %wb_hbm.1) | copy-start | bytes 22276
  4.8 0.7 %copy-start.4 = (f32[1024]{0:T(1024)S(1)}, f32[1024]{0:T(1024)}, u32[]{:S(2)}) copy-start(f32[1024]{0:T(1024)} %param.7) | copy-start | bytes 12292

commit v2 on v1

--- a/solution.py
+++ b/solution.py
@@ -39,11 +39,11 @@
 def kernel(
     cfg,
     h_hbm, gain_hbm, ng_hbm, kg_hbm, wb_hbm, cnt_hbm,
-    hg_hbm, wg_ref,
+    hg_ref, wg_ref,
     h2, gainv, ngv, kg2, wbv, cntv,
     sq, pj, rs, nrm, onehot, onehot_t, jcol,
-    gathered, send, recv, zsend, zrecv, wfull, p_own, p_send, p_recv, hgv,
-    local_sem, sq_s, sq_r, sib_s, sib_r, c1_s, c1_r, b_s, b_r, c2_s, c2_r, pj_s, pj_r, z_s, z_r,
+    gathered, kept, y_send, y_recv, x_send, x_recv, zsend, zrecv, wfull, product, p_recv,
+    local_sem, sq_s, sq_r, sib_s, sib_r, c1_s, c1_r, by_s, by_r, bx_s, bx_r, c2_s, c2_r, pj_s, pj_r, z_s, z_r,
 ):
     outer, inner, quarters, chips = cfg["outer"], cfg["inner"], cfg["quarters"], cfg["chips"]
     slots, most, group_blocks, blocks = cfg["slots"], cfg["most"], cfg["group_blocks"], cfg["blocks"]
@@ -69,7 +69,13 @@
 
     z_peers = [(k, lax.rem(x + k, outer)) for k in range(1, outer)]
     z_peers.sort(key=lambda p: -min(p[0], outer - p[0]))
-    chip_peers = [(k, lax.rem(chip + k, chips)) for k in range(1, chips)]
+    half = chips // 2
+    column = lax.rem(chip, half)
+    own_base = chip - column
+    other_base = lax.rem(own_base + half, chips)
+    across = other_base + column
+    y_peer = at(x, across, core, q)
+    x_peers = [(k, own_base + lax.rem(column + k, half)) for k in range(1, half)]
     gz_peers = [
         (dc * quarters + dq - 1, lax.rem(core + dc, CORES), lax.rem(q + dq, quarters))
         for dc in range(CORES)
@@ -89,7 +95,7 @@
         copy.start()
     barrier = pltpu.get_barrier_semaphore()
     peers = [at(zx, chip, core, q) for _, zx in z_peers]
-    peers += [at(x, other_chip, core, q) for _, other_chip in chip_peers]
+    peers += [y_peer] + [at(x, to, core, q) for _, to in x_peers]
     peers += [at(x, chip, gcore, gq) for _, gcore, gq in gz_peers]
     for peer in peers:
         pl.semaphore_signal(barrier, inc=1, device_id=peer, device_id_type=MESH)
@@ -196,46 +202,58 @@
             scaled = h2[c, :, g].astype(F32) * rs[c] * gainv[:, g]
             nrm[c * LANES : (c + 1) * LANES, g] = scaled.astype(BF16)
 
+    for copy in c1_copies:
+        copy.wait_recv()
+    own_slots = gathered.at[chip]
+    c2_y = push(own_slots, own_slots, c2_s.at[0], c2_r.at[0], y_peer)
+    c2_copies = [
+        push(own_slots, own_slots, c2_s.at[k], c2_r.at[k], at(x, to, core, q)) for k, to in x_peers
+    ]
+
     step = outer // BATCHES
-    b_copies = []
+    by_copies = []
     for batch in range(BATCHES):
         for z in range(batch * step, (batch + 1) * step):
             lane0, _ = windows(z)
             picked = nt_dot(onehot[z], nrm[:, lane0 : lane0 + lane_window]).astype(BF16)
-            product = jnp.dot(picked, kg2[...], preferred_element_type=F32)
+            spread = jnp.dot(picked, kg2[...], preferred_element_type=F32)
             piece_of = jcol[:, z : z + 1]
-            value = product[:, :LANES]
+            value = spread[:, :LANES]
             for j in range(1, pieces):
-                value = jnp.where(piece_of == j, product[:, j * LANES : (j + 1) * LANES], value)
-            send[:, z] = value.astype(BF16).reshape(chips, slots, LANES)
+                value = jnp.where(piece_of == j, spread[:, j * LANES : (j + 1) * LANES], value)
+            value = value.reshape(chips, slots, LANES)
+            kept[:, z] = value
+            y_send[:, z] = value.astype(BF16)
         span = pl.ds(batch * step, step)
-        b_copies.append([
+        by_copies.append(push(
+            y_send.at[pl.ds(other_base, half), span], y_recv.at[:, span], by_s.at[batch], by_r.at[batch], y_peer
+        ))
+
+    c2_y.wait_recv()
+    c2_copies += [
+        push(
+            gathered.at[across], gathered.at[across], c2_s.at[half - 1 + k], c2_r.at[half - 1 + k],
+            at(x, to, core, q),
+        )
+        for k, to in x_peers
+    ]
+
+    bx_copies = []
+    for batch in range(BATCHES):
+        by_copies[batch].wait_recv()
+        for z in range(batch * step, (batch + 1) * step):
+            kept[chip, z] = kept[chip, z] + y_recv[column, z].astype(F32)
+            for k, to in x_peers:
+                total = kept[to, z] + y_recv[to - own_base, z].astype(F32)
+                x_send[k - 1, z] = total.astype(BF16)
+        span = pl.ds(batch * step, step)
+        bx_copies.append([
             push(
-                send.at[to, span], recv.at[k - 1, span], b_s.at[k - 1, batch], b_r.at[k - 1, batch],
+                x_send.at[k - 1, span], x_recv.at[k - 1, span], bx_s.at[k - 1, batch], bx_r.at[k - 1, batch],
                 at(x, to, core, q),
             )
-            for k, to in chip_peers
+            for k, to in x_peers
         ])
-
-    for copy in c1_copies:
-        copy.wait_recv()
-    c2_copies = [
-        push(gathered.at[chip], gathered.at[chip], c2_s.at[k - 1], c2_r.at[k - 1], at(x, to, core, q))
-        for k, to in chip_peers
-    ]
-
-    for batch in range(BATCHES):
-        for copy in b_copies[batch]:
-            copy.wait_recv()
-        for z in range(batch * step, (batch + 1) * step):
-            total = send[chip, z].astype(F32)
-            for k in range(1, chips):
-                total = total + recv[k - 1, z].astype(F32)
-            zsend[z] = total
-    zz_copies = [
-        push(zsend.at[zx], zrecv.at[k - 1], z_s.at[k - 1], z_r.at[k - 1], at(zx, chip, core, q))
-        for k, zx in z_peers
-    ]
 
     for copy in c2_copies:
         copy.wait_recv()
@@ -250,17 +268,36 @@
             onehot_t[z], spread, preferred_element_type=F32
         )
     weight = wfull[...].astype(BF16)
-    p_send[...] = nt_dot(kg2[other_rows], weight)
-    p_copy = push(p_send, p_recv, sib_s.at[2], sib_r.at[2], sibling)
-    p_own[...] = nt_dot(kg2[own_rows], weight)
+    product[...] = nt_dot(kg2[...], weight)
+    p_copy = push(product.at[other_rows], p_recv, sib_s.at[2], sib_r.at[2], sibling)
+
+    def z_copy(k, zx, peer):
+        return pltpu.make_async_remote_copy(
+            src_ref=zsend.at[zx], dst_ref=zrecv.at[k - 1], send_sem=z_s.at[k - 1], recv_sem=z_r.at[k - 1],
+            device_id=peer, device_id_type=MESH,
+        )
+
+    for batch in range(BATCHES):
+        for copy in bx_copies[batch]:
+            copy.wait_recv()
+        for z in range(batch * step, (batch + 1) * step):
+            total = kept[chip, z]
+            for k, _ in x_peers:
+                total = total + x_recv[k - 1, z].astype(F32)
+            zsend[z] = total
+        for z in range(batch * step, (batch + 1) * step):
+
+            @pl.when(x != z)
+            def _():
+                z_copy(lax.rem(z - x + outer, outer), z, at(z, chip, core, q)).start()
 
     loads[5].wait()
     p_copy.wait_recv()
     partial = jnp.zeros((LANES, LANES), F32)
     for g in groups:
-        dnorm = ngv[:, g].astype(F32) + (p_own[:, g] + p_recv[:, g])
+        dnorm = ngv[:, g].astype(F32) + (product[own_rows, g] + p_recv[:, g])
         gained = gainv[:, g] * dnorm
-        p_own[:, g] = gained
+        p_recv[:, g] = gained
         partial = partial + gained * h2[core, :, g].astype(F32)
     row = jnp.sum(jnp.transpose(partial), axis=0, keepdims=True)
     pj[q] = jnp.broadcast_to(row, (8, LANES))
@@ -276,18 +313,17 @@
     rstd = rs[core]
     coefficient = rstd * rstd * rstd * as_column(proj) / model_width
     for g in groups:
-        grad = p_own[:, g] * rstd - h2[core, :, g].astype(F32) * coefficient
-        hgv[:, g] = grad.astype(BF16)
-    store = pltpu.make_async_copy(hgv, hg_hbm, local_sem.at[6])
-    store.start()
-
-    for copy in zz_copies:
-        copy.wait_recv()
+        grad = p_recv[:, g] * rstd - h2[core, :, g].astype(F32) * coefficient
+        hg_ref[:, g] = grad.astype(BF16)
+
+    for k, zx in z_peers:
+        z_copy(k, zx, at(zx, chip, core, q)).wait_recv()
     total = zsend[x]
     for k in range(1, outer):
         total = total + zrecv[k - 1]
     wg_ref[0, 0] = total[:most]
-    store.wait()
+    for k, zx in z_peers:
+        z_copy(k, zx, at(zx, chip, core, q)).wait_send()
     for copy in sends:
         copy.wait_send()
 
@@ -302,6 +338,8 @@
     group_blocks = (blocks + outer - 1) // outer
     slots = round_up(most, 32)
     chips = inner // CORES
+    half = chips // 2
+    lines = max(half - 1, 1)
     per_group = chips * slots
     padded_outer = round_up(outer, 16)
     span = (group_blocks + pieces - 1) // pieces + 1
@@ -317,11 +355,11 @@
     hg, wg = pl.pallas_call(
         functools.partial(kernel, cfg),
         out_shape=(
-            jax.ShapeDtypeStruct((tokens, rows), BF16),
-            jax.ShapeDtypeStruct(weight_blocks.shape, F32),
+            pltpu.VMEM((tokens, rows), BF16),
+            pltpu.VMEM(weight_blocks.shape, F32),
         ),
-        in_specs=[pl.BlockSpec(memory_space=pl.ANY)] * 6,
-        out_specs=(pl.BlockSpec(memory_space=pl.ANY), pl.BlockSpec(memory_space=pltpu.VMEM)),
+        in_specs=[pl.BlockSpec(memory_space=pltpu.HBM)] * 6,
+        out_specs=(pl.BlockSpec(memory_space=pltpu.VMEM), pl.BlockSpec(memory_space=pltpu.VMEM)),
         scratch_shapes=[
             vmem((CORES, tokens, rows), BF16),
             vmem((1, rows), F32),
@@ -337,26 +375,28 @@
             vmem((outer, cfg["row_window"], per_group), BF16),
             vmem((per_group, padded_outer), jnp.int32),
             vmem((chips, outer, slots, LANES), BF16),
+            vmem((chips, outer, slots, LANES), F32),
             vmem((chips, outer, slots, LANES), BF16),
-            vmem((chips - 1, outer, slots, LANES), BF16),
+            vmem((half, outer, slots, LANES), BF16),
+            vmem((lines, outer, slots, LANES), BF16),
+            vmem((lines, outer, slots, LANES), BF16),
             vmem((outer, slots, LANES), F32),
             vmem((outer - 1, slots, LANES), F32),
             vmem((rows, width), F32),
+            vmem((CORES * tokens, rows), F32),
             vmem((tokens, rows), F32),
-            vmem((tokens, rows), F32),
-            vmem((tokens, rows), F32),
-            vmem((tokens, rows), BF16),
-            dma((7,)),
+            dma((6,)),
             dma((CORES * quarters - 1,)), dma((CORES * quarters - 1,)),
             dma((3,)), dma((3,)),
             dma((outer - 1,)), dma((outer - 1,)),
-            dma((chips - 1, BATCHES)), dma((chips - 1, BATCHES)),
+            dma((BATCHES,)), dma((BATCHES,)),
+            dma((lines, BATCHES)), dma((lines, BATCHES)),
             dma((chips - 1,)), dma((chips - 1,)),
-            dma((quarters - 1,)), dma((quarters - 1,)),
+            dma((max(quarters - 1, 1),)), dma((max(quarters - 1, 1),)),
             dma((outer - 1,)), dma((outer - 1,)),
         ],
         compiler_params=pltpu.CompilerParams(
-            collective_id=0, has_side_effects=True, vmem_limit_bytes=48 * 1024 * 1024
+            collective_id=0, has_side_effects=True, vmem_limit_bytes=60_000_000
         ),
         name="key_projection_backward",
     )(hidden_in, norm_gain.reshape(1, rows), normed_grad, key_grad, weight_blocks, block_count)

time: 60.6 us -> 50.1 us (0.83)
  Pallas kernels: 53.5 us -> 48 us
  local copies, waits for them, and re-layouts: 6.18 us -> 1.32 us
    pallas_call x1, Pallas kernels: 53.5 us -> 48 us  [shards(): pl.pallas_call(functools.partial(kernel, cfg), out_shape=(pltpu.VMEM((tok...]
    unnamed x13 -> x1, local copies, waits for them, and re-layouts: 5.56 us -> 0.71 us
where the time goes in v2:
time: 50.1 us; the launch traced here: 50 us
  Pallas kernels  48 us (96%)
  local copies, waits for them, and re-layouts  1.32 us (3%)
  between operations  0.64 us (1%)
    pallas_call x1, Pallas kernels, shards(): pl.pallas_call(functools.partial(kernel, cfg), out_shape=(pltpu.VMEM((tok...  48 us

profile of v2, /device:TPU:1, one launch (start us, length us, event | category | flops | bytes accessed | tf_op | source)
XLA Modules:
  0.0 50.0 jit_solution(10615140969023058996)
XLA Ops:
  0.6 48.0 %key_projection_backward.1 = (bf16[128,1024]{1,0:T(8,128)(2,1)S(1)}, f32[1,1,29,128]{3,2,1,0:T(8,128)S(1)}) custom-call(bf16[128,1024]{1,0:T(8,128)(2,1)} %h_hbm.1, f32[1,1024]{1,0:T(1,128)} %bitcast.1, bf16[128,1024]{1,0:T(8,128)(2,1)} %ng_hbm.1, bf16[128,512]{1,0:T(8,128)(2,1)} %kg_hbm.1, bf16[1,1,29,128]{3,2,1,0:T(8,128)(2,1)} %wb_hbm.1, s32[1,192]{1,0:T(1,128)} %cnt_hbm.1), custom_call_target="tpu_custom_call" | custom-call | tf_op jit(solution)/shard_map/key_projection_backward/pallas_call | solution.py:355
  48.6 0.7 %copy.10 = bf16[128,1024]{1,0:T(8,128)(2,1)} copy(bf16[128,1024]{1,0:T(8,128)(2,1)S(1)} %get-tuple-element.4) | data formatting | bytes 524288
  49.3 0.6 %copy.8 = f32[1,1,29,128]{3,1,2,0:T(1,128)} copy(f32[1,1,29,128]{3,2,1,0:T(8,128)S(1)} %get-tuple-element.3) | data formatting | bytes 29696 | tf_op jit(solution)/shard_map/key_projection_backward/pallas_call | solution.py:355

commit v3 on v2

v3 whole, which is shorter than its diff:
```python
import functools

import jax
import jax.numpy as jnp
from jax import lax
from jax.experimental import pallas as pl
from jax.experimental.pallas import tpu as pltpu
from jax.sharding import PartitionSpec as P

EPS = 1e-06
LANES = 128
CORES = 2
F32 = jnp.float32
BF16 = jnp.bfloat16
MESH = pl.DeviceIdType.MESH
BATCHES = (3, 3, 3, 2, 1)


def round_up(value, step):
    return (value + step - 1) // step * step


def iota(shape, dim):
    return lax.broadcasted_iota(jnp.int32, shape, dim)


def nt_dot(a, b):
    return lax.dot_general(a, b, (((1,), (1,)), ((), ())), preferred_element_type=F32)


def as_column(row):
    return jnp.transpose(jnp.broadcast_to(row, (LANES, LANES)))


def lane_groups(rows):
    return [slice(g * LANES, (g + 1) * LANES) for g in range(rows // LANES)]


def kernel(
    cfg,
    h_hbm, gain_hbm, ng_hbm, kg_hbm, wb_hbm, cnt_hbm,
    hg_ref, wg_ref,
    h2, gainv, ngv, kg2, wbv, cntv,
    sq, pj, rs, nrm, onehot, onehot_t, piece_of,
    gathered, kept, y_send, y_recv, x_send, x_recv, zsend, zrecv, wfull, product, p_recv,
    local_sem, send_sem, sib_sem, recv_sem, by_sem, bx_sem,
):
    outer, inner, quarters, chips = cfg["outer"], cfg["inner"], cfg["quarters"], cfg["chips"]
    slots, most, group_blocks, blocks = cfg["slots"], cfg["most"], cfg["group_blocks"], cfg["blocks"]
    rows, width, pieces, model_width = cfg["rows"], cfg["width"], cfg["pieces"], cfg["model_width"]
    lane_window, row_window, padded_outer = cfg["lane_window"], cfg["row_window"], cfg["padded_outer"]
    per_group = chips * slots
    owners = outer * inner
    slot_bits = slots.bit_length() - 1
    inner_bits = inner.bit_length() - 1
    piece_bits = pieces.bit_length() - 1

    x = lax.axis_index("gx")
    y = lax.axis_index("gy")
    q = lax.axis_index("gz")
    core = lax.rem(y, CORES)
    chip = y // CORES
    other = 1 - core
    own_rows = pl.ds(pl.multiple_of(core * LANES, LANES), LANES)
    other_rows = pl.ds(pl.multiple_of(other * LANES, LANES), LANES)

    def at(gx, gchip, gcore, gz):
        return (gx, gchip * CORES + gcore, gz)

    z_peers = [(k, lax.rem(x + k, outer)) for k in range(1, outer)]
    z_peers.sort(key=lambda p: -min(p[0], outer - p[0]))
    half = chips // 2
    column = lax.rem(chip, half)
    own_base = chip - column
    other_base = lax.rem(own_base + half, chips)
    across = other_base + column
    y_peer = at(x, across, core, q)
    x_peers = [(k, own_base + lax.rem(column + k, half)) for k in range(1, half)]
    SQ, C1, BY, BX, C2, PJ, ZZ = range(7)
    C2_Y, C2_OWN, C2_ACROSS = range(7, 10)
    gz_peers = [
        (dc * quarters + dq - 1, lax.rem(core + dc, CORES), lax.rem(q + dq, quarters))
        for dc in range(CORES)
        for dq in range(quarters)
        if dc or dq
    ]

    loads = [
        pltpu.make_async_copy(h_hbm, h2.at[core], local_sem.at[0]),
        pltpu.make_async_copy(cnt_hbm, cntv, local_sem.at[1]),
        pltpu.make_async_copy(wb_hbm, wbv, local_sem.at[2]),
        pltpu.make_async_copy(kg_hbm, kg2.at[own_rows], local_sem.at[3]),
        pltpu.make_async_copy(gain_hbm, gainv, local_sem.at[4]),
        pltpu.make_async_copy(ng_hbm, ngv, local_sem.at[5]),
    ]
    for copy in loads:
        copy.start()
    barrier = pltpu.get_barrier_semaphore()
    peers = [at(zx, chip, core, q) for _, zx in z_peers]
    peers += [y_peer] + [at(x, to, core, q) for _, to in x_peers]
    peers += [at(x, chip, gcore, gq) for _, gcore, gq in gz_peers]
    for peer in peers:
        pl.semaphore_signal(barrier, inc=1, device_id=peer, device_id_type=MESH)

    groups = lane_groups(rows)

    loads[0].wait()
    partial = jnp.zeros((LANES, LANES), F32)
    for g in groups:
        piece = h2[core, :, g].astype(F32)
        partial = partial + piece * piece
    row = jnp.sum(jnp.transpose(partial), axis=0, keepdims=True)
    sq[core * quarters + q] = jnp.broadcast_to(row, (8, LANES))

    loads[2].wait()
    own_blocks = jnp.concatenate(
        [wbv[0, 0].astype(F32), jnp.zeros((slots - most, LANES), F32)], axis=0
    )
    gathered[chip, x] = own_blocks.astype(BF16)
    loads[3].wait()

    pl.semaphore_wait(barrier, len(peers))

    def push(src, dst, sender, receiver, peer):
        copy = pltpu.make_async_remote_copy(
            src_ref=src, dst_ref=dst, send_sem=sender, recv_sem=receiver, device_id=peer, device_id_type=MESH
        )
        copy.start()

    def arrived(like, semaphore):
        pltpu.make_async_copy(like, like, semaphore).wait()

    own_sq = sq.at[core * quarters + q]
    for _, gcore, gq in gz_peers:
        push(own_sq, own_sq, send_sem.at[SQ], recv_sem.at[SQ], at(x, chip, gcore, gq))
    own_blocks = gathered.at[chip, x]
    for _, zx in z_peers:
        push(own_blocks, own_blocks, send_sem.at[C1], recv_sem.at[C1], at(zx, chip, core, q))
    sibling = at(x, chip, other, q)
    own_keys, own_hidden = kg2.at[own_rows], h2.at[core]
    push(own_keys, own_keys, sib_sem.at[0], sib_sem.at[1], sibling)
    push(own_hidden, own_hidden, sib_sem.at[2], sib_sem.at[3], sibling)

    loads[1].wait()
    loads[4].wait()
    counts = cntv[...].astype(F32)
    owner_of = iota((padded_outer, owners), 1)
    of_group = (owner_of >> inner_bits) == iota((padded_outer, owners), 0)
    by_group = jnp.where(of_group, jnp.broadcast_to(counts, (padded_outer, owners)), 0.0).astype(BF16)

    def placed(shape, slot_dim, owner_dim):
        slot = iota(shape, slot_dim)
        holder = (slot >> slot_bits) * CORES + core
        within = iota(shape, owner_dim) & (inner - 1)
        before = jnp.where(within < holder, 1.0, 0.0).astype(BF16)
        mine = jnp.where(within == holder, 1.0, 0.0).astype(BF16)
        return before, mine

    before, mine = placed((per_group, owners), 0, 1)
    start_c = nt_dot(before, by_group).astype(jnp.int32)
    count_c = nt_dot(mine, by_group).astype(jnp.int32)
    within_c = iota((per_group, padded_outer), 0) & (slots - 1)
    block_c = start_c + within_c + group_blocks * iota((per_group, padded_outer), 1)
    block_c = jnp.where(within_c < count_c, block_c, -pieces)
    row_c = block_c >> piece_bits
    piece_c = block_c & (pieces - 1)
    start_r = nt_dot(by_group, before).astype(jnp.int32)
    count_r = nt_dot(by_group, mine).astype(jnp.int32)
    within_r = iota((padded_outer, per_group), 1) & (slots - 1)
    block_r = start_r + within_r + group_blocks * iota((padded_outer, per_group), 0)
    block_r = jnp.where(within_r < count_r, block_r, -pieces)
    row_r = block_r >> piece_bits

    def first_lane(z):
        return group_blocks * z // pieces // LANES * LANES

    def first_row(z):
        return min(group_blocks * z // pieces // 8 * 8, rows - row_window)

    for z in range(outer):
        hit = row_c[:, z : z + 1] == first_lane(z) + iota((per_group, lane_window), 1)
        onehot[z] = jnp.where(hit, 1.0, 0.0).astype(BF16)
        hit = row_r[z : z + 1, :] == first_row(z) + iota((row_window, per_group), 0)
        onehot_t[z] = jnp.where(hit, 1.0, 0.0).astype(BF16)
        piece_of[z] = jnp.broadcast_to(piece_c[:, z : z + 1], (per_group, LANES))
    nrm[:, rows:] = jnp.zeros((CORES * LANES, LANES), BF16)
    wfull[...] = jnp.zeros_like(wfull)

    arrived(sq.at[pl.ds(0, len(gz_peers))], recv_sem.at[SQ])
    arrived(own_keys, sib_sem.at[1])
    arrived(own_hidden, sib_sem.at[3])
    for c in range(CORES):
        total = sq[c * quarters, 0:1]
        for other_q in range(1, quarters):
            total = total + sq[c * quarters + other_q, 0:1]
        rs[c] = as_column(lax.rsqrt(total / model_width + EPS))
        for g in groups:
            scaled = h2[c, :, g].astype(F32) * rs[c] * gainv[:, g]
            nrm[c * LANES : (c + 1) * LANES, g] = scaled.astype(BF16)

    offsets = sorted(range(outer), key=lambda k: -min(k, outer - k))
    ends = [sum(BATCHES[: b + 1]) for b in range(len(BATCHES))]
    spans = [(end - size, size) for end, size in zip(ends, BATCHES)]

    def slot_gradients(batch):
        start, size = spans[batch]
        for n in range(start, start + size):
            z = lax.rem(x + offsets[n], outer)
            lanes = pl.ds(pl.multiple_of(first_lane(z), LANES), lane_window)
            picked = nt_dot(onehot[z], nrm[:, lanes]).astype(BF16)
            spread = jnp.dot(picked, kg2[...], preferred_element_type=F32)
            value = spread[:, :LANES]
            for j in range(1, pieces):
                value = jnp.where(piece_of[z] == j, spread[:, j * LANES : (j + 1) * LANES], value)
            value = value.reshape(chips, slots, LANES)
            kept[:, n] = value
            y_send[:, n] = value.astype(BF16)
        span = pl.ds(start, size)
        push(
            y_send.at[pl.ds(other_base, half), span], y_recv.at[:, span], send_sem.at[BY], by_sem.at[batch], y_peer
        )

    def along_x(batch):
        start, size = spans[batch]
        span = pl.ds(start, size)
        arrived(y_recv.at[:, span], by_sem.at[batch])
        for n in range(start, start + size):
            kept[chip, n] = kept[chip, n] + y_recv[column, n].astype(F32)
            for k, to in x_peers:
                total = kept[to, n] + y_recv[to - own_base, n].astype(F32)
                x_send[k - 1, n] = total.astype(BF16)
        for k, to in x_peers:
            push(
                x_send.at[k - 1, span], x_recv.at[k - 1, span], send_sem.at[BX], bx_sem.at[batch],
                at(x, to, core, q),
            )

    def along_z(batch):
        start, size = spans[batch]
        span = pl.ds(start, size)
        if x_peers:
            arrived(x_recv.at[:, span], bx_sem.at[batch])
        for n in range(start, start + size):
            total = kept[chip, n]
            for k, _ in x_peers:
                total = total + x_recv[k - 1, n].astype(F32)
            zsend[n] = total
            if offsets[n]:
                push(
                    zsend.at[n], zrecv.at[n], send_sem.at[ZZ], recv_sem.at[ZZ],
                    at(lax.rem(x + offsets[n], outer), chip, core, q),
                )

    if z_peers:
        arrived(gathered.at[chip, pl.ds(0, outer - 1)], recv_sem.at[C1])
    def share(source, receiver, peers):
        held = gathered.at[source]
        for to in peers:
            push(held, held, send_sem.at[C2], recv_sem.at[receiver], at(x, to, core, q))

    along = [to for _, to in x_peers]
    share(chip, C2_Y, [across])
    share(chip, C2_OWN, along)
    batches = range(len(BATCHES))
    for batch in batches:
        slot_gradients(batch)
    arrived(gathered.at[across], recv_sem.at[C2_Y])
    share(across, C2_ACROSS, along)
    for batch in batches:
        along_x(batch)
    for batch in batches[:1]:
        along_z(batch)
    if along:
        arrived(gathered.at[pl.ds(0, len(along))], recv_sem.at[C2_OWN])
        arrived(gathered.at[pl.ds(0, len(along))], recv_sem.at[C2_ACROSS])
    for z in range(outer):
        row0 = first_row(z)
        values = gathered[:, z].reshape(per_group, LANES)
        spread = jnp.concatenate(
            [jnp.where(piece_of[z] == j, values, jnp.zeros_like(values)) for j in range(pieces)], axis=1
        )
        wfull[row0 : row0 + row_window, :] += jnp.dot(
            onehot_t[z], spread, preferred_element_type=F32
        )
    weight = wfull[...].astype(BF16)
    product[...] = nt_dot(kg2[...], weight)
    push(product.at[other_rows], p_recv, sib_sem.at[4], sib_sem.at[5], sibling)
    for batch in batches[1:3]:
        along_z(batch)

    loads[5].wait()
    arrived(p_recv, sib_sem.at[5])
    partial = jnp.zeros((LANES, LANES), F32)
    for g in groups:
        dnorm = ngv[:, g].astype(F32) + (product[own_rows, g] + p_recv[:, g])
        gained = gainv[:, g] * dnorm
        p_recv[:, g] = gained
        partial = partial + gained * h2[core, :, g].astype(F32)
    row = jnp.sum(jnp.transpose(partial), axis=0, keepdims=True)
    pj[q] = jnp.broadcast_to(row, (8, LANES))
    own_pj = pj.at[q]
    for dq in range(1, quarters):
        push(own_pj, own_pj, send_sem.at[PJ], recv_sem.at[PJ], at(x, chip, core, lax.rem(q + dq, quarters)))
    for batch in batches[3:]:
        along_z(batch)
    if quarters > 1:
        arrived(pj.at[pl.ds(0, quarters - 1)], recv_sem.at[PJ])
    proj = pj[0, 0:1]
    for other_q in range(1, quarters):
        proj = proj + pj[other_q, 0:1]
    rstd = rs[core]
    coefficient = rstd * rstd * rstd * as_column(proj) / model_width
    for g in groups:
        grad = p_recv[:, g] * rstd - h2[core, :, g].astype(F32) * coefficient
        hg_ref[:, g] = grad.astype(BF16)

    if z_peers:
        arrived(zrecv, recv_sem.at[ZZ])
    total = zsend[outer - 1]
    for n in range(outer - 1):
        total = total + zrecv[n]
    wg_ref[0, 0] = total[:most]
    arrived(sq.at[pl.ds(0, len(gz_peers))], send_sem.at[SQ])
    arrived(own_keys, sib_sem.at[0])
    arrived(own_hidden, sib_sem.at[2])
    arrived(p_recv, sib_sem.at[4])
    arrived(y_recv, send_sem.at[BY])
    arrived(gathered.at[pl.ds(0, chips - 1)], send_sem.at[C2])
    if x_peers:
        arrived(x_recv, send_sem.at[BX])
    if z_peers:
        arrived(gathered.at[0, pl.ds(0, outer - 1)], send_sem.at[C1])
        arrived(zrecv, send_sem.at[ZZ])
    if quarters > 1:
        arrived(pj.at[pl.ds(0, quarters - 1)], send_sem.at[PJ])


def finish(most, hg_ref, wg_ref, hg_out, wg_out, lines, sem):
    wide = pltpu.make_async_copy(hg_ref, hg_out, sem.at[0])
    wide.start()
    for row in range(most):
        lines[row] = wg_ref[0, 0, row : row + 1, :]
    narrow = pltpu.make_async_copy(lines, wg_out, sem.at[1])
    narrow.start()
    wide.wait()
    narrow.wait()


def shards(hidden_in, norm_gain, normed_grad, key_grad, weight_blocks, block_count):
    outer, inner, quarters = lax.axis_size("gx"), lax.axis_size("gy"), lax.axis_size("gz")
    tokens, rows = hidden_in.shape
    width = key_grad.shape[1]
    most = weight_blocks.shape[2]
    blocks = rows * width // LANES
    pieces = width // LANES
    group_blocks = (blocks + outer - 1) // outer
    slots = round_up(most, 32)
    chips = inner // CORES
    half = chips // 2
    lines = max(half - 1, 1)
    per_group = chips * slots
    padded_outer = round_up(outer, 16)
    span = (group_blocks + pieces - 1) // pieces + 1
    cfg = dict(
        outer=outer, inner=inner, quarters=quarters, chips=chips, slots=slots, most=most,
        group_blocks=group_blocks, blocks=blocks, rows=rows, width=width, pieces=pieces,
        model_width=rows * quarters, padded_outer=padded_outer,
        lane_window=min(rows, round_up(span + LANES - 1, LANES)),
        row_window=min(rows, round_up(span + 7, 8)),
    )
    vmem = pltpu.VMEM
    dma = pltpu.SemaphoreType.DMA
    hg, wg = pl.pallas_call(
        functools.partial(kernel, cfg),
        out_shape=(
            pltpu.VMEM((tokens, rows), BF16),
            pltpu.VMEM(weight_blocks.shape, F32),
        ),
        in_specs=[pl.BlockSpec(memory_space=pltpu.HBM)] * 6,
        out_specs=(pl.BlockSpec(memory_space=pltpu.VMEM), pl.BlockSpec(memory_space=pltpu.VMEM)),
        scratch_shapes=[
            vmem((CORES, tokens, rows), BF16),
            vmem((1, rows), F32),
            vmem((tokens, rows), BF16),
            vmem((CORES * tokens, width), BF16),
            vmem(weight_blocks.shape, BF16),
            vmem(block_count.shape, jnp.int32),
            vmem((CORES * quarters, 8, LANES), F32),
            vmem((quarters, 8, LANES), F32),
            vmem((CORES, LANES, LANES), F32),
            vmem((CORES * tokens, rows + LANES), BF16),
            vmem((outer, per_group, cfg["lane_window"]), BF16),
            vmem((outer, cfg["row_window"], per_group), BF16),
            vmem((outer, per_group, LANES), jnp.int32),
            vmem((chips, outer, slots, LANES), BF16),
            vmem((chips, outer, slots, LANES), F32),
            vmem((chips, outer, slots, LANES), BF16),
            vmem((half, outer, slots, LANES), BF16),
            vmem((lines, outer, slots, LANES), BF16),
            vmem((lines, outer, slots, LANES), BF16),
            vmem((outer, slots, LANES), F32),
            vmem((max(outer - 1, 1), slots, LANES), F32),
            vmem((rows, width), F32),
            vmem((CORES * tokens, rows), F32),
            vmem((tokens, rows), F32),
            dma((6,)), dma((7,)), dma((6,)), dma((10,)), dma((len(BATCHES),)), dma((len(BATCHES),)),
        ],
        compiler_params=pltpu.CompilerParams(
            collective_id=0, has_side_effects=True, vmem_limit_bytes=60_000_000
        ),
        name="key_projection_backward",
    )(hidden_in, norm_gain.reshape(1, rows), normed_grad, key_grad, weight_blocks, block_count)
    hg, wg = pl.pallas_call(
        functools.partial(finish, most),
        out_shape=(
            jax.ShapeDtypeStruct((tokens, rows), BF16),
            jax.ShapeDtypeStruct((most, 1, LANES), F32),
        ),
        in_specs=[pl.BlockSpec(memory_space=pltpu.VMEM)] * 2,
        out_specs=[pl.BlockSpec(memory_space=pltpu.HBM)] * 2,
        scratch_shapes=[vmem((most, 1, LANES), F32), dma((2,))],
        compiler_params=pltpu.CompilerParams(vmem_limit_bytes=2 * 1024 * 1024),
        name="write_results",
    )(hg, wg)
    return hg, wg.reshape(weight_blocks.shape)


def solution(mesh):
    placed = (
        P(("gx", "gy"), "gz"),
        P("gz"),
        P(("gx", "gy"), "gz"),
        P(("gx", "gy"), None),
        P(("gx", "gy"), "gz", None, None),
        P("gz", None),
    )
    return jax.shard_map(
        shards,
        mesh=mesh,
        in_specs=placed,
        out_specs=(P(("gx", "gy"), "gz"), P(("gx", "gy"), "gz", None, None)),
        check_vma=False,
    )
```

time: 50.1 us -> 48.5 us (0.968)
  local copies, waits for them, and re-layouts: 1.32 us -> 0 us
    pallas_call x1, Pallas kernels: 48 us -> 47 us  [shards(): pl.pallas_call(functools.partial(kernel, cfg), out_shape=(pltpu.VMEM((tok...]
    pallas_call x0 -> x1, Pallas kernels: none -> 0.72 us  [shards(): pl.pallas_call(functools.partial(finish, most), out_shape=(jax.ShapeDtype...]
    unnamed x1 -> x0, local copies, waits for them, and re-layouts: 0.71 us -> none
    pallas_call x1 -> x0, local copies, waits for them, and re-layouts: 0.62 us -> none  [shards(): pl.pallas_call(functools.partial(kernel, cfg), out_shape=(pltpu.VMEM((tok...]
where the time goes in v3:
time: 48.5 us; the launch traced here: 48.3 us
  Pallas kernels  47.7 us (98%)
  between operations  0.64 us (1%)
    pallas_call x1, Pallas kernels, shards(): pl.pallas_call(functools.partial(kernel, cfg), out_shape=(pltpu.VMEM((tok...  47 us

profile of v3, /device:TPU:1, one launch (start us, length us, event | category | flops | bytes accessed | tf_op | source)
XLA Modules:
  0.0 48.3 jit_solution(12294729503895467655)
XLA Ops:
  0.6 47.0 %key_projection_backward.1 = (bf16[128,1024]{1,0:T(8,128)(2,1)S(1)}, f32[1,1,29,128]{3,2,1,0:T(8,128)S(1)}) custom-call(bf16[128,1024]{1,0:T(8,128)(2,1)} %h_hbm.1, f32[1,1024]{1,0:T(1,128)} %bitcast.4, bf16[128,1024]{1,0:T(8,128)(2,1)} %ng_hbm.1, bf16[128,512]{1,0:T(8,128)(2,1)} %kg_hbm.1, bf16[1,1,29,128]{3,2,1,0:T(8,128)(2,1)} %wb_hbm.1, s32[1,192]{1,0:T(1,128)} %cnt_hbm.1), custom_call_target="tpu_custom_call" | custom-call | tf_op jit(solution)/shard_map/key_projection_backward/pallas_call | solution.py:373
  47.6 0.7 %write_results.1 = (bf16[128,1024]{1,0:T(8,128)(2,1)}, f32[29,1,128]{2,1,0:T(1,128)}) custom-call(bf16[128,1024]{1,0:T(8,128)(2,1)S(1)} %get-tuple-element.6.hg_ref, f32[1,1,29,128]{3,2,1,0:T(8,128)S(1)} %get-tuple-element.7.wg_ref), custom_call_target="tpu_custom_call" | custom-call | tf_op jit(solution)/shard_map/write_results/pallas_call | solution.py:413

commit v4 on v3

--- a/solution.py
+++ b/solution.py
@@ -42,7 +42,7 @@
     hg_ref, wg_ref,
     h2, gainv, ngv, kg2, wbv, cntv,
     sq, pj, rs, nrm, onehot, onehot_t, piece_of,
-    gathered, kept, y_send, y_recv, x_send, x_recv, zsend, zrecv, wfull, product, p_recv,
+    proj_early, pj_other, gathered, kept, y_send, y_recv, x_send, x_recv, zsend, zrecv, wfull, product, p_recv,
     local_sem, send_sem, sib_sem, recv_sem, by_sem, bx_sem,
 ):
     outer, inner, quarters, chips = cfg["outer"], cfg["inner"], cfg["quarters"], cfg["chips"]
@@ -68,7 +68,7 @@
         return (gx, gchip * CORES + gcore, gz)
 
     z_peers = [(k, lax.rem(x + k, outer)) for k in range(1, outer)]
-    z_peers.sort(key=lambda p: -min(p[0], outer - p[0]))
+    z_peers.sort(key=lambda p: min(p[0], outer - p[0]))
     half = chips // 2
     column = lax.rem(chip, half)
     own_base = chip - column
@@ -77,13 +77,18 @@
     y_peer = at(x, across, core, q)
     x_peers = [(k, own_base + lax.rem(column + k, half)) for k in range(1, half)]
     SQ, C1, BY, BX, C2, PJ, ZZ = range(7)
-    C2_Y, C2_OWN, C2_ACROSS = range(7, 10)
+    C1_FAR, C2_Y, C2_Y_FAR, C2_OWN, C2_ACROSS = range(7, 12)
     gz_peers = [
         (dc * quarters + dq - 1, lax.rem(core + dc, CORES), lax.rem(q + dq, quarters))
         for dc in range(CORES)
         for dq in range(quarters)
         if dc or dq
     ]
+
+    offsets = sorted(range(outer), key=lambda k: -min(k, outer - k))
+    place = [offsets.index(k) for k in range(outer)]
+    far = sum(min(k, outer - k) > 3 for k in offsets)
+    far_planes, near_planes = pl.ds(0, far), pl.ds(far, outer - far)
 
     loads = [
         pltpu.make_async_copy(h_hbm, h2.at[core], local_sem.at[0]),
@@ -116,7 +121,7 @@
     own_blocks = jnp.concatenate(
         [wbv[0, 0].astype(F32), jnp.zeros((slots - most, LANES), F32)], axis=0
     )
-    gathered[chip, x] = own_blocks.astype(BF16)
+    gathered[chip, outer - 1] = own_blocks.astype(BF16)
     loads[3].wait()
 
     pl.semaphore_wait(barrier, len(peers))
@@ -133,9 +138,13 @@
     own_sq = sq.at[core * quarters + q]
     for _, gcore, gq in gz_peers:
         push(own_sq, own_sq, send_sem.at[SQ], recv_sem.at[SQ], at(x, chip, gcore, gq))
-    own_blocks = gathered.at[chip, x]
-    for _, zx in z_peers:
-        push(own_blocks, own_blocks, send_sem.at[C1], recv_sem.at[C1], at(zx, chip, core, q))
+    own_blocks = gathered.at[chip, outer - 1]
+    for k, zx in z_peers:
+        spot = place[outer - k]
+        push(
+            own_blocks, gathered.at[chip, spot], send_sem.at[C1], recv_sem.at[C1_FAR if spot < far else C1],
+            at(zx, chip, core, q),
+        )
     sibling = at(x, chip, other, q)
     own_keys, own_hidden = kg2.at[own_rows], h2.at[core]
     push(own_keys, own_keys, sib_sem.at[0], sib_sem.at[1], sibling)
@@ -175,7 +184,7 @@
         return group_blocks * z // pieces // LANES * LANES
 
     def first_row(z):
-        return min(group_blocks * z // pieces // 8 * 8, rows - row_window)
+        return group_blocks * z // pieces // 8 * 8
 
     for z in range(outer):
         hit = row_c[:, z : z + 1] == first_lane(z) + iota((per_group, lane_window), 1)
@@ -185,6 +194,19 @@
         piece_of[z] = jnp.broadcast_to(piece_c[:, z : z + 1], (per_group, LANES))
     nrm[:, rows:] = jnp.zeros((CORES * LANES, LANES), BF16)
     wfull[...] = jnp.zeros_like(wfull)
+
+    loads[5].wait()
+    partial = jnp.zeros((LANES, LANES), F32)
+    for g in groups:
+        partial = partial + gainv[:, g] * ngv[:, g].astype(F32) * h2[core, :, g].astype(F32)
+    proj_early[...] = partial
+
+    def share(source, receiver, peers, planes):
+        held = gathered.at[source, planes]
+        for to in peers:
+            push(held, held, send_sem.at[C2], recv_sem.at[receiver], at(x, to, core, q))
+
+    along = [to for _, to in x_peers]
 
     arrived(sq.at[pl.ds(0, len(gz_peers))], recv_sem.at[SQ])
     arrived(own_keys, sib_sem.at[1])
@@ -198,7 +220,6 @@
             scaled = h2[c, :, g].astype(F32) * rs[c] * gainv[:, g]
             nrm[c * LANES : (c + 1) * LANES, g] = scaled.astype(BF16)
 
-    offsets = sorted(range(outer), key=lambda k: -min(k, outer - k))
     ends = [sum(BATCHES[: b + 1]) for b in range(len(BATCHES))]
     spans = [(end - size, size) for end, size in zip(ends, BATCHES)]
 
@@ -251,63 +272,73 @@
                     at(lax.rem(x + offsets[n], outer), chip, core, q),
                 )
 
-    if z_peers:
-        arrived(gathered.at[chip, pl.ds(0, outer - 1)], recv_sem.at[C1])
-    def share(source, receiver, peers):
-        held = gathered.at[source]
-        for to in peers:
-            push(held, held, send_sem.at[C2], recv_sem.at[receiver], at(x, to, core, q))
-
-    along = [to for _, to in x_peers]
-    share(chip, C2_Y, [across])
-    share(chip, C2_OWN, along)
+    if outer - far > 1:
+        arrived(gathered.at[chip, pl.ds(far, outer - far - 1)], recv_sem.at[C1])
+    share(chip, C2_Y, [across], near_planes)
+    share(chip, C2_OWN, along, near_planes)
     batches = range(len(BATCHES))
-    for batch in batches:
+    for batch in batches[:1]:
         slot_gradients(batch)
-    arrived(gathered.at[across], recv_sem.at[C2_Y])
-    share(across, C2_ACROSS, along)
-    for batch in batches:
+    if far:
+        arrived(gathered.at[chip, far_planes], recv_sem.at[C1_FAR])
+        share(chip, C2_Y_FAR, [across], far_planes)
+        share(chip, C2_OWN, along, far_planes)
+    for batch in batches[1:2]:
+        slot_gradients(batch)
+    arrived(gathered.at[across, near_planes], recv_sem.at[C2_Y])
+    share(across, C2_ACROSS, along, near_planes)
+    for batch in batches[2:]:
+        slot_gradients(batch)
+    along_x(0)
+    if far:
+        arrived(gathered.at[across, far_planes], recv_sem.at[C2_Y_FAR])
+        share(across, C2_ACROSS, along, far_planes)
+    for batch in batches[1:]:
         along_x(batch)
-    for batch in batches[:1]:
-        along_z(batch)
+        if batch == 3:
+            along_z(0)
     if along:
         arrived(gathered.at[pl.ds(0, len(along))], recv_sem.at[C2_OWN])
         arrived(gathered.at[pl.ds(0, len(along))], recv_sem.at[C2_ACROSS])
-    for z in range(outer):
-        row0 = first_row(z)
-        values = gathered[:, z].reshape(per_group, LANES)
+    for n in range(outer):
+        z = lax.rem(x + offsets[n], outer)
+        spread_rows = pl.ds(pl.multiple_of(first_row(z), 8), row_window)
+        values = gathered[:, n].reshape(per_group, LANES)
         spread = jnp.concatenate(
             [jnp.where(piece_of[z] == j, values, jnp.zeros_like(values)) for j in range(pieces)], axis=1
         )
-        wfull[row0 : row0 + row_window, :] += jnp.dot(
+        wfull[spread_rows, :] += jnp.dot(
             onehot_t[z], spread, preferred_element_type=F32
         )
-    weight = wfull[...].astype(BF16)
+    weight = wfull[:rows].astype(BF16)
     product[...] = nt_dot(kg2[...], weight)
     push(product.at[other_rows], p_recv, sib_sem.at[4], sib_sem.at[5], sibling)
-    for batch in batches[1:3]:
+    partial = proj_early[...]
+    part_other = jnp.zeros((LANES, LANES), F32)
+    for g in groups:
+        partial = partial + gainv[:, g] * h2[core, :, g].astype(F32) * product[own_rows, g]
+        part_other = part_other + gainv[:, g] * h2[other, :, g].astype(F32) * product[other_rows, g]
+    own_pj = pj.at[core * quarters + q]
+    pj[core * quarters + q] = jnp.broadcast_to(jnp.sum(jnp.transpose(partial), axis=0, keepdims=True), (8, LANES))
+    pj_other[...] = jnp.broadcast_to(jnp.sum(jnp.transpose(part_other), axis=0, keepdims=True), (8, LANES))
+    for m, gcore, gq in gz_peers:
+        push(
+            own_pj if m < quarters - 1 else pj_other, own_pj, send_sem.at[PJ], recv_sem.at[PJ],
+            at(x, chip, gcore, gq),
+        )
+    for batch in batches[0 if len(batches) < 4 else 1 : 3]:
         along_z(batch)
 
-    loads[5].wait()
     arrived(p_recv, sib_sem.at[5])
-    partial = jnp.zeros((LANES, LANES), F32)
     for g in groups:
         dnorm = ngv[:, g].astype(F32) + (product[own_rows, g] + p_recv[:, g])
-        gained = gainv[:, g] * dnorm
-        p_recv[:, g] = gained
-        partial = partial + gained * h2[core, :, g].astype(F32)
-    row = jnp.sum(jnp.transpose(partial), axis=0, keepdims=True)
-    pj[q] = jnp.broadcast_to(row, (8, LANES))
-    own_pj = pj.at[q]
-    for dq in range(1, quarters):
-        push(own_pj, own_pj, send_sem.at[PJ], recv_sem.at[PJ], at(x, chip, core, lax.rem(q + dq, quarters)))
+        p_recv[:, g] = gainv[:, g] * dnorm
     for batch in batches[3:]:
         along_z(batch)
-    if quarters > 1:
-        arrived(pj.at[pl.ds(0, quarters - 1)], recv_sem.at[PJ])
+    arrived(pj.at[pl.ds(0, len(gz_peers))], recv_sem.at[PJ])
     proj = pj[0, 0:1]
-    for other_q in range(1, quarters):
-        proj = proj + pj[other_q, 0:1]
+    for m in range(1, CORES * quarters):
+        proj = proj + pj[m, 0:1]
     rstd = rs[core]
     coefficient = rstd * rstd * rstd * as_column(proj) / model_width
     for g in groups:
@@ -331,8 +362,7 @@
     if z_peers:
         arrived(gathered.at[0, pl.ds(0, outer - 1)], send_sem.at[C1])
         arrived(zrecv, send_sem.at[ZZ])
-    if quarters > 1:
-        arrived(pj.at[pl.ds(0, quarters - 1)], send_sem.at[PJ])
+    arrived(pj.at[pl.ds(0, len(gz_peers))], send_sem.at[PJ])
 
 
 def finish(most, hg_ref, wg_ref, hg_out, wg_out, lines, sem):
@@ -386,12 +416,14 @@
             vmem(weight_blocks.shape, BF16),
             vmem(block_count.shape, jnp.int32),
             vmem((CORES * quarters, 8, LANES), F32),
-            vmem((quarters, 8, LANES), F32),
+            vmem((CORES * quarters, 8, LANES), F32),
             vmem((CORES, LANES, LANES), F32),
             vmem((CORES * tokens, rows + LANES), BF16),
             vmem((outer, per_group, cfg["lane_window"]), BF16),
             vmem((outer, cfg["row_window"], per_group), BF16),
             vmem((outer, per_group, LANES), jnp.int32),
+            vmem((LANES, LANES), F32),
+            vmem((8, LANES), F32),
             vmem((chips, outer, slots, LANES), BF16),
             vmem((chips, outer, slots, LANES), F32),
             vmem((chips, outer, slots, LANES), BF16),
@@ -400,10 +432,10 @@
             vmem((lines, outer, slots, LANES), BF16),
             vmem((outer, slots, LANES), F32),
             vmem((max(outer - 1, 1), slots, LANES), F32),
-            vmem((rows, width), F32),
+            vmem((rows + cfg["row_window"], width), F32),
             vmem((CORES * tokens, rows), F32),
             vmem((tokens, rows), F32),
-            dma((6,)), dma((7,)), dma((6,)), dma((10,)), dma((len(BATCHES),)), dma((len(BATCHES),)),
+            dma((6,)), dma((7,)), dma((6,)), dma((12,)), dma((len(BATCHES),)), dma((len(BATCHES),)),
         ],
         compiler_params=pltpu.CompilerParams(
             collective_id=0, has_side_effects=True, vmem_limit_bytes=60_000_000

time: 48.5 us -> 46.5 us (0.959)
  Pallas kernels: 47.7 us -> 45.7 us
    pallas_call x1, Pallas kernels: 47 us -> 45 us  [shards(): pl.pallas_call(functools.partial(kernel, cfg), out_shape=(pltpu.VMEM((tok...]
where the time goes in v4:
time: 46.5 us; the launch traced here: 46.4 us
  Pallas kernels  45.7 us (98%)
  between operations  0.64 us (1%)
    pallas_call x1, Pallas kernels, shards(): pl.pallas_call(functools.partial(kernel, cfg), out_shape=(pltpu.VMEM((tok...  45 us

profile of v4, /device:TPU:1, one launch (start us, length us, event | category | flops | bytes accessed | tf_op | source)
XLA Modules:
  0.0 46.4 jit_solution(17257989760448271413)
XLA Ops:
  0.6 45.0 %key_projection_backward.1 = (bf16[128,1024]{1,0:T(8,128)(2,1)S(1)}, f32[1,1,29,128]{3,2,1,0:T(8,128)S(1)}) custom-call(bf16[128,1024]{1,0:T(8,128)(2,1)} %h_hbm.1, f32[1,1024]{1,0:T(1,128)} %bitcast.4, bf16[128,1024]{1,0:T(8,128)(2,1)} %ng_hbm.1, bf16[128,512]{1,0:T(8,128)(2,1)} %kg_hbm.1, bf16[1,1,29,128]{3,2,1,0:T(8,128)(2,1)} %wb_hbm.1, s32[1,192]{1,0:T(1,128)} %cnt_hbm.1), custom_call_target="tpu_custom_call" | custom-call | tf_op jit(solution)/shard_map/key_projection_backward/pallas_call | solution.py:403
  45.7 0.7 %write_results.1 = (bf16[128,1024]{1,0:T(8,128)(2,1)}, f32[29,1,128]{2,1,0:T(1,128)}) custom-call(bf16[128,1024]{1,0:T(8,128)(2,1)S(1)} %get-tuple-element.6.hg_ref, f32[1,1,29,128]{3,2,1,0:T(8,128)S(1)} %get-tuple-element.7.wg_ref), custom_call_target="tpu_custom_call" | custom-call | tf_op jit(solution)/shard_map/write_results/pallas_call | solution.py:445

commit v5 on v4

--- a/solution.py
+++ b/solution.py
@@ -77,7 +77,7 @@
     y_peer = at(x, across, core, q)
     x_peers = [(k, own_base + lax.rem(column + k, half)) for k in range(1, half)]
     SQ, C1, BY, BX, C2, PJ, ZZ = range(7)
-    C1_FAR, C2_Y, C2_Y_FAR, C2_OWN, C2_ACROSS = range(7, 12)
+    C1_FAR, C2_Y, C2_Y_FAR, OWN, OWN_FAR, ACROSS, ACROSS_FAR, PASS_OWN, PASS_OWN_FAR, PASS_ACROSS = range(7, 17)
     gz_peers = [
         (dc * quarters + dq - 1, lax.rem(core + dc, CORES), lax.rem(q + dq, quarters))
         for dc in range(CORES)
@@ -207,6 +207,16 @@
             push(held, held, send_sem.at[C2], recv_sem.at[receiver], at(x, to, core, q))
 
     along = [to for _, to in x_peers]
+    ring = half == 4
+    beside = [to for k, to in x_peers if not ring or k != 2]
+    right, left = lax.rem(column + 1, half), lax.rem(column + half - 1, half)
+
+    def pass_on(came_in, planes, source, receiver, to):
+        if beside:
+            arrived(gathered.at[pl.ds(0, len(beside)), planes], recv_sem.at[came_in])
+        if ring:
+            share(source, receiver, [to], planes)
+
 
     arrived(sq.at[pl.ds(0, len(gz_peers))], recv_sem.at[SQ])
     arrived(own_keys, sib_sem.at[1])
@@ -275,31 +285,38 @@
     if outer - far > 1:
         arrived(gathered.at[chip, pl.ds(far, outer - far - 1)], recv_sem.at[C1])
     share(chip, C2_Y, [across], near_planes)
-    share(chip, C2_OWN, along, near_planes)
+    share(chip, OWN, beside, near_planes)
     batches = range(len(BATCHES))
     for batch in batches[:1]:
         slot_gradients(batch)
     if far:
         arrived(gathered.at[chip, far_planes], recv_sem.at[C1_FAR])
         share(chip, C2_Y_FAR, [across], far_planes)
-        share(chip, C2_OWN, along, far_planes)
+        share(chip, OWN_FAR, beside, far_planes)
     for batch in batches[1:2]:
         slot_gradients(batch)
     arrived(gathered.at[across, near_planes], recv_sem.at[C2_Y])
-    share(across, C2_ACROSS, along, near_planes)
+    share(across, ACROSS, beside, near_planes)
+    pass_on(OWN, near_planes, own_base + right, PASS_OWN, own_base + left)
     for batch in batches[2:]:
         slot_gradients(batch)
     along_x(0)
     if far:
         arrived(gathered.at[across, far_planes], recv_sem.at[C2_Y_FAR])
-        share(across, C2_ACROSS, along, far_planes)
+        share(across, ACROSS_FAR, along, far_planes)
+        pass_on(OWN_FAR, far_planes, own_base + left, PASS_OWN_FAR, own_base + right)
+    pass_on(ACROSS, near_planes, other_base + right, PASS_ACROSS, own_base + left)
     for batch in batches[1:]:
         along_x(batch)
         if batch == 3:
             along_z(0)
-    if along:
-        arrived(gathered.at[pl.ds(0, len(along))], recv_sem.at[C2_OWN])
-        arrived(gathered.at[pl.ds(0, len(along))], recv_sem.at[C2_ACROSS])
+    if along and far:
+        arrived(gathered.at[pl.ds(0, len(along)), far_planes], recv_sem.at[ACROSS_FAR])
+    if ring:
+        arrived(gathered.at[0, near_planes], recv_sem.at[PASS_OWN])
+        arrived(gathered.at[0, near_planes], recv_sem.at[PASS_ACROSS])
+        if far:
+            arrived(gathered.at[0, far_planes], recv_sem.at[PASS_OWN_FAR])
     for n in range(outer):
         z = lax.rem(x + offsets[n], outer)
         spread_rows = pl.ds(pl.multiple_of(first_row(z), 8), row_window)
@@ -310,6 +327,8 @@
         wfull[spread_rows, :] += jnp.dot(
             onehot_t[z], spread, preferred_element_type=F32
         )
+    for batch in batches[1:2]:
+        along_z(batch)
     weight = wfull[:rows].astype(BF16)
     product[...] = nt_dot(kg2[...], weight)
     push(product.at[other_rows], p_recv, sib_sem.at[4], sib_sem.at[5], sibling)
@@ -326,7 +345,7 @@
             own_pj if m < quarters - 1 else pj_other, own_pj, send_sem.at[PJ], recv_sem.at[PJ],
             at(x, chip, gcore, gq),
         )
-    for batch in batches[0 if len(batches) < 4 else 1 : 3]:
+    for batch in [*batches[: 1 if len(batches) < 4 else 0], *batches[2:3]]:
         along_z(batch)
 
     arrived(p_recv, sib_sem.at[5])
@@ -435,7 +454,7 @@
             vmem((rows + cfg["row_window"], width), F32),
             vmem((CORES * tokens, rows), F32),
             vmem((tokens, rows), F32),
-            dma((6,)), dma((7,)), dma((6,)), dma((12,)), dma((len(BATCHES),)), dma((len(BATCHES),)),
+            dma((6,)), dma((7,)), dma((6,)), dma((17,)), dma((len(BATCHES),)), dma((len(BATCHES),)),
         ],
         compiler_params=pltpu.CompilerParams(
             collective_id=0, has_side_effects=True, vmem_limit_bytes=60_000_000

time: 46.5 us -> 45.8 us (0.985)
  Pallas kernels: 45.7 us -> 45.1 us
    pallas_call x1, Pallas kernels: 45 us -> 44.3 us  [shards(): pl.pallas_call(functools.partial(kernel, cfg), out_shape=(pltpu.VMEM((tok...]
where the time goes in v5:
time: 45.8 us; the launch traced here: 45.7 us
  Pallas kernels  45.1 us (98%)
  between operations  0.64 us (1%)
    pallas_call x1, Pallas kernels, shards(): pl.pallas_call(functools.partial(kernel, cfg), out_shape=(pltpu.VMEM((tok...  44.3 us

profile of v5, /device:TPU:1, one launch (start us, length us, event | category | flops | bytes accessed | tf_op | source)
XLA Modules:
  0.0 45.7 jit_solution(7318904606901612612)
XLA Ops:
  0.6 44.3 %key_projection_backward.1 = (bf16[128,1024]{1,0:T(8,128)(2,1)S(1)}, f32[1,1,29,128]{3,2,1,0:T(8,128)S(1)}) custom-call(bf16[128,1024]{1,0:T(8,128)(2,1)} %h_hbm.1, f32[1,1024]{1,0:T(1,128)} %bitcast.4, bf16[128,1024]{1,0:T(8,128)(2,1)} %ng_hbm.1, bf16[128,512]{1,0:T(8,128)(2,1)} %kg_hbm.1, bf16[1,1,29,128]{3,2,1,0:T(8,128)(2,1)} %wb_hbm.1, s32[1,192]{1,0:T(1,128)} %cnt_hbm.1), custom_call_target="tpu_custom_call" | custom-call | tf_op jit(solution)/shard_map/key_projection_backward/pallas_call | solution.py:422
  45.0 0.7 %write_results.1 = (bf16[128,1024]{1,0:T(8,128)(2,1)}, f32[29,1,128]{2,1,0:T(1,128)}) custom-call(bf16[128,1024]{1,0:T(8,128)(2,1)S(1)} %get-tuple-element.6.hg_ref, f32[1,1,29,128]{3,2,1,0:T(8,128)S(1)} %get-tuple-element.7.wg_ref), custom_call_target="tpu_custom_call" | custom-call | tf_op jit(solution)/shard_map/write_results/pallas_call | solution.py:464

commit v6 on v5

--- a/solution.py
+++ b/solution.py
@@ -218,6 +218,10 @@
             share(source, receiver, [to], planes)
 
 
+    if outer - far > 1:
+        arrived(gathered.at[chip, pl.ds(far, outer - far - 1)], recv_sem.at[C1])
+    share(chip, C2_Y, [across], near_planes)
+    share(chip, OWN, beside, near_planes)
     arrived(sq.at[pl.ds(0, len(gz_peers))], recv_sem.at[SQ])
     arrived(own_keys, sib_sem.at[1])
     arrived(own_hidden, sib_sem.at[3])
@@ -282,10 +286,6 @@
                     at(lax.rem(x + offsets[n], outer), chip, core, q),
                 )
 
-    if outer - far > 1:
-        arrived(gathered.at[chip, pl.ds(far, outer - far - 1)], recv_sem.at[C1])
-    share(chip, C2_Y, [across], near_planes)
-    share(chip, OWN, beside, near_planes)
     batches = range(len(BATCHES))
     for batch in batches[:1]:
         slot_gradients(batch)
@@ -306,27 +306,28 @@
         share(across, ACROSS_FAR, along, far_planes)
         pass_on(OWN_FAR, far_planes, own_base + left, PASS_OWN_FAR, own_base + right)
     pass_on(ACROSS, near_planes, other_base + right, PASS_ACROSS, own_base + left)
+    def weight_rows(planes):
+        for n in planes:
+            z = lax.rem(x + offsets[n], outer)
+            spread_rows = pl.ds(pl.multiple_of(first_row(z), 8), row_window)
+            values = gathered[:, n].reshape(per_group, LANES)
+            spread = jnp.concatenate(
+                [jnp.where(piece_of[z] == j, values, jnp.zeros_like(values)) for j in range(pieces)], axis=1
+            )
+            wfull[spread_rows, :] += jnp.dot(onehot_t[z], spread, preferred_element_type=F32)
+
     for batch in batches[1:]:
         along_x(batch)
         if batch == 3:
             along_z(0)
-    if along and far:
-        arrived(gathered.at[pl.ds(0, len(along)), far_planes], recv_sem.at[ACROSS_FAR])
+            if far:
+                arrived(gathered.at[pl.ds(0, len(along)), far_planes], recv_sem.at[ACROSS_FAR])
+                arrived(gathered.at[0, far_planes], recv_sem.at[PASS_OWN_FAR])
+            weight_rows(range(far))
     if ring:
         arrived(gathered.at[0, near_planes], recv_sem.at[PASS_OWN])
         arrived(gathered.at[0, near_planes], recv_sem.at[PASS_ACROSS])
-        if far:
-            arrived(gathered.at[0, far_planes], recv_sem.at[PASS_OWN_FAR])
-    for n in range(outer):
-        z = lax.rem(x + offsets[n], outer)
-        spread_rows = pl.ds(pl.multiple_of(first_row(z), 8), row_window)
-        values = gathered[:, n].reshape(per_group, LANES)
-        spread = jnp.concatenate(
-            [jnp.where(piece_of[z] == j, values, jnp.zeros_like(values)) for j in range(pieces)], axis=1
-        )
-        wfull[spread_rows, :] += jnp.dot(
-            onehot_t[z], spread, preferred_element_type=F32
-        )
+    weight_rows(range(far, outer))
     for batch in batches[1:2]:
         along_z(batch)
     weight = wfull[:rows].astype(BF16)

time: 45.8 us -> 45.8 us (level)
  no operation moved by 1% of the time
where the time goes in v6:
time: 45.8 us; the launch traced here: 45.6 us
  Pallas kernels  45 us (98%)
  between operations  0.64 us (1%)
    pallas_call x1, Pallas kernels, shards(): pl.pallas_call(functools.partial(kernel, cfg), out_shape=(pltpu.VMEM((tok...  44.2 us

profile of v6, /device:TPU:1, one launch (start us, length us, event | category | flops | bytes accessed | tf_op | source)
XLA Modules:
  0.0 45.6 jit_solution(6052660682442590269)
XLA Ops:
  0.6 44.2 %key_projection_backward.1 = (bf16[128,1024]{1,0:T(8,128)(2,1)S(1)}, f32[1,1,29,128]{3,2,1,0:T(8,128)S(1)}) custom-call(bf16[128,1024]{1,0:T(8,128)(2,1)} %h_hbm.1, f32[1,1024]{1,0:T(1,128)} %bitcast.4, bf16[128,1024]{1,0:T(8,128)(2,1)} %ng_hbm.1, bf16[128,512]{1,0:T(8,128)(2,1)} %kg_hbm.1, bf16[1,1,29,128]{3,2,1,0:T(8,128)(2,1)} %wb_hbm.1, s32[1,192]{1,0:T(1,128)} %cnt_hbm.1), custom_call_target="tpu_custom_call" | custom-call | tf_op jit(solution)/shard_map/key_projection_backward/pallas_call | solution.py:423
  44.9 0.7 %write_results.1 = (bf16[128,1024]{1,0:T(8,128)(2,1)}, f32[29,1,128]{2,1,0:T(1,128)}) custom-call(bf16[128,1024]{1,0:T(8,128)(2,1)S(1)} %get-tuple-element.6.hg_ref, f32[1,1,29,128]{3,2,1,0:T(8,128)S(1)} %get-tuple-element.7.wg_ref), custom_call_target="tpu_custom_call" | custom-call | tf_op jit(solution)/shard_map/write_results/pallas_call | solution.py:465

commit v7 on v6

--- a/solution.py
+++ b/solution.py
@@ -332,7 +332,6 @@
         along_z(batch)
     weight = wfull[:rows].astype(BF16)
     product[...] = nt_dot(kg2[...], weight)
-    push(product.at[other_rows], p_recv, sib_sem.at[4], sib_sem.at[5], sibling)
     partial = proj_early[...]
     part_other = jnp.zeros((LANES, LANES), F32)
     for g in groups:
@@ -346,6 +345,7 @@
             own_pj if m < quarters - 1 else pj_other, own_pj, send_sem.at[PJ], recv_sem.at[PJ],
             at(x, chip, gcore, gq),
         )
+    push(product.at[other_rows], p_recv, sib_sem.at[4], sib_sem.at[5], sibling)
     for batch in [*batches[: 1 if len(batches) < 4 else 0], *batches[2:3]]:
         along_z(batch)
 

time: 45.8 us -> 45.8 us (level)
  no operation moved by 1% of the time
where the time goes in v7:
time: 45.8 us; the launch traced here: 45.6 us
  Pallas kernels  45 us (98%)
  between operations  0.64 us (1%)
    pallas_call x1, Pallas kernels, shards(): pl.pallas_call(functools.partial(kernel, cfg), out_shape=(pltpu.VMEM((tok...  44.3 us

profile of v7, /device:TPU:1, one launch (start us, length us, event | category | flops | bytes accessed | tf_op | source)
XLA Modules:
  0.0 45.6 jit_solution(3891083319916753918)
XLA Ops:
  0.6 44.3 %key_projection_backward.1 = (bf16[128,1024]{1,0:T(8,128)(2,1)S(1)}, f32[1,1,29,128]{3,2,1,0:T(8,128)S(1)}) custom-call(bf16[128,1024]{1,0:T(8,128)(2,1)} %h_hbm.1, f32[1,1024]{1,0:T(1,128)} %bitcast.4, bf16[128,1024]{1,0:T(8,128)(2,1)} %ng_hbm.1, bf16[128,512]{1,0:T(8,128)(2,1)} %kg_hbm.1, bf16[1,1,29,128]{3,2,1,0:T(8,128)(2,1)} %wb_hbm.1, s32[1,192]{1,0:T(1,128)} %cnt_hbm.1), custom_call_target="tpu_custom_call" | custom-call | tf_op jit(solution)/shard_map/key_projection_backward/pallas_call | solution.py:423
  44.9 0.7 %write_results.1 = (bf16[128,1024]{1,0:T(8,128)(2,1)}, f32[29,1,128]{2,1,0:T(1,128)}) custom-call(bf16[128,1024]{1,0:T(8,128)(2,1)S(1)} %get-tuple-element.6.hg_ref, f32[1,1,29,128]{3,2,1,0:T(8,128)S(1)} %get-tuple-element.7.wg_ref), custom_call_target="tpu_custom_call" | custom-call | tf_op jit(solution)/shard_map/write_results/pallas_call | solution.py:465
